TPU v7x, 256 devices: a whole 4x4x8 slice. The times are simulated.
256 devices in a mesh: seq: 32 (over z, y), tensor: 8 (over x, core).
Axes of the slice: x: 4, y: 4, z: 8, core: 2. Of those that a mesh axis runs over, the one named last changes fastest.
Arguments:
- layer_input: bfloat16 [8192, 4096], P('seq', 'tensor'), may hold values from -6 to 6
- norm_gain: float32 [4096], replicated, may hold values from 0.1 to 1.9
- in_weights: bfloat16 [2, 4096, 2048], P(None, None, 'tensor'), may hold values from -0.09375 to 0.09375
- conv_weight: float32 [4, 2048], P(None, 'tensor'), may hold values from -4 to 4
- conv_bias: float32 [2048], P('tensor'), may hold values from -3 to 3
- gate_weights: bfloat16 [2, 8, 256, 256], P(None, 'tensor'), may hold values from -0.375 to 0.375
- gate_bias: float32 [2, 2048], P(None, 'tensor'), may hold values from -4 to 4
- decay_rate: float32 [2048], P('tensor'), may hold values from 1e-06 to 0.03, as said below
- out_weight: bfloat16 [2048, 4096], P('tensor'), may hold values from -0.1875 to 0.1875
- mlp_gain: float32 [4096], replicated, may hold values from 0.1 to 1.9
- mlp_in: bfloat16 [2, 4096, 6144], P(None, 'seq', 'tensor'), may hold values from -0.09375 to 0.09375
- mlp_out: bfloat16 [6144, 4096], P('tensor', 'seq'), may hold values from -0.15625 to 0.15625
Outputs:
- block_output: bfloat16 [8192, 4096], P('seq', 'tensor')
Inputs may be any that keep to these rules, and one draw needn't show every extreme that they name: `decay_rate`: every rate is positive.
All inputs are finite; a program needn't handle non-finite values.
Results may differ from a plain program's by a relative error of at most 0.015.
Values may be sent and summed in bfloat16 or wider, within the bound.
A program may use at most 128 MiB of HBM per device.

v0:
```python
import jax
import jax.numpy as jnp
from jax import lax
from jax.sharding import Mesh
from jax.sharding import PartitionSpec as P

SEQ = ("seq_0", "seq_1")


def from_everyone(value, axis):
    copies = jnp.broadcast_to(value, (lax.axis_size(axis), *value.shape))
    return lax.all_to_all(copies, axis, split_axis=0, concat_axis=0, tiled=True)


def joined_along(blocks, dim):
    shape = list(blocks.shape[1:])
    shape[dim] *= blocks.shape[0]
    return jnp.moveaxis(blocks, 0, dim).reshape(shape)


def gather_directly(value, axis, dim):
    blocks = from_everyone(value, axis)
    return joined_along(blocks, dim)


def shifted(value, axis, steps):
    count = lax.axis_size(axis)
    first, last = (max(0, -steps), min(count, count - steps))
    return lax.ppermute(value, axis, [(source, source + steps) for source in range(first, last)])


def side_by_side(arrays, axis, dim, along):
    ends, at = ([], 0)
    for a in arrays[:-1]:
        at += a.shape[along]
        ends.append(at)
    both = jnp.concatenate(arrays, axis=along)
    return tuple(jnp.split(lax.all_gather(both, axis, axis=dim, tiled=True), ends, axis=along))


def in_blocks(value, dim, size):
    shape = value.shape
    blocks = value.reshape(*shape[:dim], size, shape[dim] // size, *shape[dim + 1 :])
    return jnp.moveaxis(blocks, dim, 0)


def summed_on_arrival(value, axis, dim):
    size = lax.axis_size(axis)
    blocks = lax.all_to_all(in_blocks(value, dim, size), axis, 0, 0, tiled=True)
    return jnp.sum(blocks.astype(jnp.float32), axis=0)


def whole_of(value, axes, dim):
    filled = value
    for number in range(len(axes) - 1, -1, -1):
        filled = lax.all_gather(filled, axes[number], axis=dim, tiled=True)
    return filled


def rms_scale(rows, gain):
    values = rows.astype(jnp.float32)
    mean_square = jnp.mean(values * values, axis=-1, keepdims=True)
    return (values * lax.rsqrt(mean_square + 1e-06) * gain).astype(jnp.bfloat16)


def chain_step(earlier, later):
    return (earlier[0] * later[0], later[0] * earlier[1] + later[1])


def shards(
    layer_input,
    norm_gain,
    in_weights,
    conv_weight,
    conv_bias,
    gate_weights,
    gate_bias,
    decay_rate,
    out_weight,
    mlp_gain,
    mlp_in,
    mlp_out,
):
    whole_rows = gather_directly(layer_input, "tensor", 1)
    normed = rms_scale(whole_rows, norm_gain)
    branch_x = jnp.dot(normed, in_weights[0], preferred_element_type=jnp.float32).astype(
        jnp.bfloat16
    )
    branch_y = jax.nn.gelu(
        jnp.dot(normed, in_weights[1], preferred_element_type=jnp.float32), approximate=True
    )
    num_tokens = branch_x.shape[0]
    rim_rows = conv_weight.shape[0] - 1
    earlier_rows = shifted(branch_x[num_tokens - rim_rows :], SEQ, 1)
    padded = jnp.concatenate([earlier_rows, branch_x], axis=0).astype(jnp.float32)
    convolved = jnp.zeros(branch_x.shape, jnp.float32) + conv_bias
    for tap_index in range(conv_weight.shape[0]):
        start_row = rim_rows - tap_index
        convolved = convolved + conv_weight[tap_index] * padded[start_row : start_row + num_tokens]
    conv_out = convolved.astype(jnp.bfloat16)
    local_blocks = gate_weights.shape[1]
    block_width = gate_weights.shape[2]
    blocks_in = conv_out.reshape(num_tokens, local_blocks, block_width)
    gate_pre = jnp.einsum(
        "tnc,knce->ktne", blocks_in, gate_weights, preferred_element_type=jnp.float32
    )
    gate_pre = gate_pre.reshape(2, num_tokens, local_blocks * block_width) + gate_bias[:, None, :]
    log_decay = -8.0 * jax.nn.sigmoid(gate_pre[0]) * decay_rate
    decay = jnp.exp(log_decay)
    driven = (
        conv_out.astype(jnp.float32)
        * jax.nn.sigmoid(gate_pre[1])
        * jnp.sqrt(-jnp.expm1(2.0 * log_decay))
    )
    cum_decay, cum_state = lax.associative_scan(chain_step, (decay, driven), axis=0)
    table_decay, table_state = side_by_side((cum_decay[-1:], cum_state[-1:]), SEQ, 0, 1)
    prefix_decay, prefix_state = lax.associative_scan(
        chain_step, (table_decay, table_state), axis=0
    )
    position = lax.axis_index(SEQ)
    previous = lax.dynamic_index_in_dim(
        prefix_state, jnp.maximum(position - 1, 0), 0, keepdims=False
    )
    carried = jnp.where(position > 0, previous, jnp.zeros_like(previous))
    state = cum_decay * carried + cum_state
    mixed = (state * branch_y).astype(jnp.bfloat16)
    partial_sums = jnp.dot(mixed, out_weight, preferred_element_type=jnp.float32)
    own_share = summed_on_arrival(partial_sums.astype(jnp.bfloat16), "tensor", 1)
    residual = (layer_input.astype(jnp.float32) + own_share).astype(jnp.bfloat16)
    mid_full = gather_directly(residual, "tensor", 1)
    mlp_normed = rms_scale(mid_full, mlp_gain)
    gate_up = jnp.einsum(
        "tr,krf->ktf",
        mlp_normed,
        lax.all_gather(mlp_in, SEQ, axis=1, tiled=True),
        preferred_element_type=jnp.float32,
    )
    hidden = (jax.nn.gelu(gate_up[0], approximate=True) * gate_up[1]).astype(jnp.bfloat16)
    down_terms = jnp.dot(hidden, whole_of(mlp_out, SEQ, 1), preferred_element_type=jnp.float32)
    down_share = summed_on_arrival(down_terms.astype(jnp.bfloat16), "tensor", 1)
    return (residual.astype(jnp.float32) + down_share).astype(jnp.bfloat16)


def solution(mesh):
    finer = Mesh(mesh.devices.reshape(8, 4, mesh.shape["tensor"]), ("seq_0", "seq_1", "tensor"))
    return jax.shard_map(
        shards,
        mesh=finer,
        in_specs=(
            P(SEQ, "tensor"),
            P(),
            P(None, None, "tensor"),
            P(None, "tensor"),
            P("tensor"),
            P(None, "tensor", None, None),
            P(None, "tensor"),
            P("tensor"),
            P("tensor", None),
            P(),
            P(None, SEQ, "tensor"),
            P("tensor", SEQ),
        ),
        out_specs=P(SEQ, "tensor"),
        check_vma=False,
    )
```

profile of v0, /device:TPU:1, one launch (start us, length us, event | category | flops | bytes accessed | tf_op | source)
XLA Modules:
  0.0 250.8 jit_solution(13636499894500978369)
XLA Ops:
  7.3 1.1 copy.17
  8.3 1.5 broadcast_in_dim.6
  9.9 7.6 %all-to-all-start = ((bf16[8,256,512]{1,2,0:T(8,128)(2,1)}), bf16[8,256,512]{1,2,0:T(8,128)(2,1)}, u32[]{:S(2)}, u32[]{:S(2)}) async-start(bf16[8,256,512]{1,2,0:T(8,128)(2,1)} %broadcast_in_dim.6), calls=%async_computation | async-start | bytes 4194304 | tf_op jit(solution)/shard_map/all_to_all | solution.py:12
  17.4 19.8 %all_gather.14 = bf16[768,512]{1,0:T(8,128)(2,1)} all-gather(bf16[768,128]{1,0:T(8,128)(2,1)S(1)} %copy-done.4), channel_id=1, replica_groups=mesh['seq_0'=8,'seq_1'=4,'tensor'=8] {'seq_1'}, dimensions={1}, use_global_device_ids=true | all-gather | bytes 983040 | tf_op jit(solution)/shard_map/all_gather | solution.py:56
  37.3 6.4 %all-to-all-done = bf16[8,256,512]{1,2,0:T(8,128)(2,1)} async-done(((bf16[8,256,512]{1,2,0:T(8,128)(2,1)}), bf16[8,256,512]{1,2,0:T(8,128)(2,1)}, u32[]{:S(2)}, u32[]{:S(2)}) %all-to-all-start) | async-done | bytes 2097184 | tf_op jit(solution)/shard_map/all_to_all | solution.py:12
  43.8 2.2 fusion
  46.0 2.1 fusion.2
  48.1 0.7 copy-done.10
  48.8 0.8 fusion.17
  49.6 1.5 collective-permute-start
  57.5 0.9 pad_maximum_fusion
  58.6 48.6 %all-gather = f32[32,1,512]{2,1,0:T(1,128)S(1)} all-gather(f32[1,1,512]{2,1,0:T(1,128)S(1)} %maximum_bitcast_fusion), channel_id=1, replica_groups=mesh['seq_0'=8,'seq_1'=4,'tensor'=8] {'seq_0','seq_1'}, dimensions={0}, use_global_device_ids=true | all-gather | bytes 67584 | tf_op jit(solution)/shard_map/all_gather | solution.py:38
  108.0 6.1 %convolution_convert_fusion = bf16[256,4096]{1,0:T(8,128)(2,1)} fusion(bf16[256,4096]{1,0:T(8,128)(2,1)S(1)} %copy-done, bf16[256,4096]{0,1:T(8,128)(2,1)} %bitcast.106, bf16[2,4096,256]{2,1,0:T(8,128)(2,1)} %param.14, f32[256,256]{1,0:T(8,128)S(1)} %pad.159, f32[256,256]{1,0:T(8,128)S(1)} %pad.160, f32[256,256]{1,0:T(8,128)S(1)} %pad.143, ...), kind=kOutput, calls=%fused_computation.2 | convolution fusion | flops 1075707904 | bytes 9438208 | tf_op jit(solution)/shard_map/dot_general | solution.py:127
  114.1 1.8 copy.31
  115.8 37.7 %all_to_all.20 = bf16[8,256,512]{2,1,0:T(8,128)(2,1)S(1)} all-to-all(bf16[8,256,512]{2,1,0:T(8,128)(2,1)S(1)} %bitcast.103), channel_id=1, replica_groups=mesh['seq_0'=8,'seq_1'=4,'tensor'=8] {'tensor'}, dimensions={0} | all-to-all | bytes 4194304 | tf_op jit(solution)/shard_map/all_to_all | solution.py:49
  154.7 30.3 %all_to_all.21 = bf16[8,256,512]{2,1,0:T(8,128)(2,1)} all-to-all(bf16[8,256,512]{2,1,0:T(8,128)(2,1)S(1)} %broadcast_in_dim.8), channel_id=1, replica_groups=mesh['seq_0'=8,'seq_1'=4,'tensor'=8] {'tensor'}, dimensions={0} | all-to-all | bytes 4194304 | tf_op jit(solution)/shard_map/all_to_all | solution.py:12
  185.1 3.9 %copy.19 = bf16[8,256,512]{1,2,0:T(8,128)(2,1)} copy(bf16[8,256,512]{2,1,0:T(8,128)(2,1)} %all_to_all.21) | data formatting | bytes 4194304 | tf_op jit(solution)/shard_map/all_to_all | solution.py:12
  189.0 2.3 multiply_reduce_fusion
  191.4 1.7 fusion.4
  193.1 9.9 %fusion.13 = f32[2,256,768]{2,1,0:T(8,128)} fusion(bf16[2,4096,768]{2,1,0:T(8,128)(2,1)} %all-gather.4.cloned.1.call-done, bf16[256,4096]{0,1:T(8,128)(2,1)} %fusion.4), kind=kOutput, calls=%fused_computation.23 | convolution fusion | flops 3221225472 | bytes 16252928 | tf_op jit(solution)/shard_map/tr,krf->ktf/dot_general | solution.py:132
  203.0 3.4 %all-gather.6.cloned.1.call-done = bf16[768,4096]{1,0:T(8,128)(2,1)} async-done(((bf16[768,512]{1,0:T(8,128)(2,1)}), bf16[768,4096]{1,0:T(8,128)(2,1)}) %all-gather.6.cloned.1.call-update) | async-done | bytes 6291472 | tf_op jit(solution)/shard_map/all_gather | solution.py:56
  206.4 5.2 %convolution_convert_fusion.1 = bf16[256,4096]{1,0:T(8,128)(2,1)S(1)} fusion(bf16[768,4096]{1,0:T(8,128)(2,1)} %all-gather.6.cloned.1.call-done, f32[2,256,768]{2,1,0:T(8,128)} %fusion.13), kind=kOutput, calls=%fused_computation.3 | convolution fusion | flops 1613627392 | bytes 9961472 | tf_op jit(solution)/shard_map/dot_general | solution.py:139
  211.9 31.1 %all_to_all.22 = bf16[8,256,512]{2,1,0:T(8,128)(2,1)S(1)} all-to-all(bf16[8,256,512]{2,1,0:T(8,128)(2,1)S(1)} %bitcast.104), channel_id=1, replica_groups=mesh['seq_0'=8,'seq_1'=4,'tensor'=8] {'tensor'}, dimensions={0} | all-to-all | bytes 4194304 | tf_op jit(solution)/shard_map/all_to_all | solution.py:49
  243.2 0.8 add_convert_fusion
  (221 shorter events, 9.0 us)
Async XLA Ops:
  6.5 101.4 %copy-start = (bf16[256,4096]{1,0:T(8,128)(2,1)S(1)}, bf16[256,4096]{1,0:T(8,128)(2,1)}, u32[]{:S(2)}) copy-start(bf16[256,4096]{1,0:T(8,128)(2,1)} %param.20) | copy-start | bytes 6291460
  6.5 186.5 %all-gather.4.cloned.1.call-start = ((), (), s32[]{:S(2)}) async-start(), calls=%async_computation.4 | async-start | bytes 12976128 | tf_op jit(solution)/shard_map/all_gather | solution.py:135
  9.9 7.6 %copy-start.4 = (bf16[768,128]{1,0:T(8,128)(2,1)S(1)}, bf16[768,128]{1,0:T(8,128)(2,1)}, u32[]{:S(2)}) copy-start(bf16[768,128]{1,0:T(8,128)(2,1)} %param.23) | copy-start | bytes 589828
  9.9 27.4 %copy-start.6 = (f32[4096]{0:T(1024)S(1)}, f32[4096]{0:T(1024)}, u32[]{:S(2)}) copy-start(f32[4096]{0:T(1024)} %param.13) | copy-start | bytes 49156
  9.9 27.5 %copy-start.7 = (f32[4,256]{1,0:T(4,128)S(1)}, f32[4,256]{1,0:T(4,128)}, u32[]{:S(2)}) copy-start(f32[4,256]{1,0:T(4,128)} %param.15) | copy-start | bytes 12292
  9.9 33.9 %all-to-all-start = ((bf16[8,256,512]{1,2,0:T(8,128)(2,1)}), bf16[8,256,512]{1,2,0:T(8,128)(2,1)}, u32[]{:S(2)}, u32[]{:S(2)}) async-start(bf16[8,256,512]{1,2,0:T(8,128)(2,1)} %broadcast_in_dim.6), calls=%async_computation | async-start | bytes 4194304 | tf_op jit(solution)/shard_map/all_to_all | solution.py:12
  17.4 189.0 %all-gather.6.cloned.1.call-start = ((), (), s32[]{:S(2)}) async-start(), calls=%async_computation.5 | async-start | bytes 7077888 | tf_op jit(solution)/shard_map/all_gather | solution.py:56
  46.0 2.9 %copy-start.10 = (bf16[2,4096,256]{2,1,0:T(8,128)(2,1)S(1)}, bf16[2,4096,256]{2,1,0:T(8,128)(2,1)}, u32[]{:S(2)}) copy-start(bf16[2,4096,256]{2,1,0:T(8,128)(2,1)} %param.14) | copy-start | bytes 12582916
  48.1 1.5 copy-start.2
  48.8 2.3 copy-start.9
  48.8 3.1 %copy-start.8 = (f32[256]{0:T(256)S(1)}, f32[256]{0:T(256)}, u32[]{:S(2)}) copy-start(f32[256]{0:T(256)} %param.16) | copy-start | bytes 3076
  48.8 3.1 %copy-start.11 = (bf16[2,1,256,256]{3,2,1,0:T(8,128)(2,1)S(1)}, bf16[2,1,256,256]{3,2,1,0:T(8,128)(2,1)}, u32[]{:S(2)}) copy-start(bf16[2,1,256,256]{3,2,1,0:T(8,128)(2,1)} %param.17) | copy-start | bytes 786436
  48.8 3.1 %copy-start.12 = (f32[2,256]{1,0:T(2,128)S(1)}, f32[2,256]{1,0:T(2,128)}, u32[]{:S(2)}) copy-start(f32[2,256]{1,0:T(2,128)} %param.18) | copy-start | bytes 6148
  49.6 2.2 collective-permute-start
  153.5 1.0 copy-start.3
  185.1 6.3 %copy-start.5 = (f32[4096]{0:T(1024)S(1)}, f32[4096]{0:T(1024)}, u32[]{:S(2)}) copy-start(f32[4096]{0:T(1024)} %param.21) | copy-start | bytes 49156
  189.0 2.4 copy-start.1
Sparse Core Ops, SparseCore 0:
  9.9 122.6 all-gather.3
  134.4 71.9 all-gather.5
where the time goes:
time: 251 us
  blocking collectives  167 us (67%)
  matrix products  22.3 us (9%)
  between operations  14.4 us (6%)
  other arithmetic  13.7 us (5%)
  local copies, waits for them, and re-layouts  12.6 us (5%)
  waiting for transfers between devices  11.3 us (5%)
  starting transfers between devices  9.08 us (4%)
    all_to_all x2, blocking collectives, summed_on_arrival(): blocks = lax.all_to_all(in_blocks(value, dim, size), axis, 0, 0, tiled=True)  68.7 us
    all_gather x1, blocking collectives, side_by_side(): lax.all_gather(both, axis, axis=dim, tiled=True)  48.6 us
    all_to_all x1, blocking collectives, from_everyone(): return lax.all_to_all(copies, axis, split_axis=0, concat_axis=0, tiled=True)  30.3 us
    all_gather x1, blocking collectives, whole_of(): filled = lax.all_gather(filled, axes[number], axis=dim, tiled=True)  19.8 us
    dot_general x1, matrix products, shards(): jnp.einsum('tr,krf->ktf', mlp_normed, lax.all_gather(mlp_in, SEQ, axis=1,...  9.92 us
    all_to_all x1, starting transfers between devices, from_everyone(): return lax.all_to_all(copies, axis, split_axis=0, concat_axis=0, tiled=True)  7.56 us
    all_to_all x1, waiting for transfers between devices, from_everyone(): return lax.all_to_all(copies, axis, split_axis=0, concat_axis=0, tiled=True)  6.42 us
    dot_general x1, matrix products, shards(): jnp.dot(mixed, out_weight, preferred_element_type=jnp.float32)  6.06 us
  transfers between devices with their start and end apart: 4, of which 3 were waited for; matrix products, arithmetic and copies ran while one was open for 16% of the time, Pallas kernels for 0%

commit v1 on v0

v1 whole, which is shorter than its diff:
```python
import functools

import jax
import jax.numpy as jnp
from jax import lax
from jax.experimental import pallas as pl
from jax.experimental.pallas import tpu as pltpu
from jax.sharding import PartitionSpec as P

NY = 4
NX = 4
EPS = 1e-06
F32 = jnp.float32
BF16 = jnp.bfloat16
MESSAGES = 200


def mod(value, size):
    return lax.rem(value + size, size)


def expm1_negated(v):
    series = 1.0 + v * (1.0 / 9.0)
    for n in range(8, 1, -1):
        series = 1.0 + v * (1.0 / n) * series
    return jnp.where(v > -0.5, -v * series, 1.0 - jnp.exp(v))


class Wire:
    def __init__(self, send, recv):
        self.send, self.recv, self.used, self.open = send, recv, 0, []

    def message(self, src, dst, landing, device):
        self.used += 1
        return Message(self, self.used - 1, src, dst, landing, device)

    def drain(self):
        for message in self.open:
            message.copy(message.dst).wait_send()


class Message:
    def __init__(self, wire, number, src, dst, landing, device):
        self.wire, self.number, self.src, self.dst, self.landing, self.device = (
            wire, number, src, dst, landing, device,
        )

    def copy(self, dst):
        return pltpu.make_async_remote_copy(
            src_ref=self.src,
            dst_ref=dst,
            send_sem=self.wire.send.at[self.number],
            recv_sem=self.wire.recv.at[self.number],
            device_id=self.device,
            device_id_type=pl.DeviceIdType.MESH,
        )

    def start(self):
        self.copy(self.dst).start()
        self.wire.open.append(self)

    def arrived(self):
        self.copy(self.landing).wait_recv()


class Spread:
    def __init__(self, wire, piece, me, device_of, own=None):
        nxt, prv, opp = mod(me + 1, 4), mod(me + 3, 4), mod(me + 2, 4)
        own = own or (lambda h: piece(me, h))
        self.na = wire.message(own(0), piece(me, 0), piece(prv, 0), device_of(nxt))
        self.nb = wire.message(own(1), piece(me, 1), piece(prv, 1), device_of(nxt))
        self.pb = wire.message(own(1), piece(me, 1), piece(nxt, 1), device_of(prv))
        self.pa = wire.message(own(0), piece(me, 0), piece(nxt, 0), device_of(prv))
        self.fn = wire.message(piece(prv, 0), piece(prv, 0), piece(opp, 0), device_of(nxt))
        self.fp = wire.message(piece(nxt, 1), piece(nxt, 1), piece(opp, 1), device_of(prv))

    def start(self):
        self.na.start()
        self.pb.start()
        self.nb.start()
        self.pa.start()

    def forward(self):
        self.na.arrived()
        self.fn.start()
        self.pb.arrived()
        self.fp.start()

    def prv_done(self):
        self.nb.arrived()

    def nxt_done(self):
        self.pa.arrived()

    def opp_done(self):
        self.fn.arrived()
        self.fp.arrived()


class Gathered:
    def __init__(self, wire, part, me, device_of, box):
        nxt, prv, opp = mod(me + 1, 4), mod(me + 3, 4), mod(me + 2, 4)
        self.part, self.me, self.nxt, self.prv, self.box = part, me, nxt, prv, box
        def send(src, slot, device):
            return wire.message(src, box.at[slot], box.at[slot], device)
        self.oa = send(part(opp, 0), 0, device_of(nxt))
        self.ob = send(part(opp, 1), 1, device_of(prv))
        self.db = send(part(nxt, 1), 2, device_of(nxt))
        self.da = send(part(prv, 0), 3, device_of(prv))
        self.ca = send(part(nxt, 0), 4, device_of(nxt))
        self.cb = send(part(prv, 1), 5, device_of(prv))

    def start_far(self):
        self.oa.start()
        self.ob.start()

    def start_next(self):
        self.db.start()

    def start_prev(self):
        self.da.start()

    def relay(self):
        for arriving, leaving, member, half, slot in (
            (self.oa, self.ca, self.nxt, 0, 0),
            (self.ob, self.cb, self.prv, 1, 1),
        ):
            arriving.arrived()
            ref = self.part(member, half)
            ref[...] = (ref[...].astype(F32) + self.box[slot].astype(F32)).astype(BF16)
            leaving.start()

    def result(self):
        self.da.arrived()
        self.ca.arrived()
        self.db.arrived()
        self.cb.arrived()
        halves = []
        for half, slots in ((0, (4, 3)), (1, (2, 5))):
            value = self.part(self.me, half)[...].astype(F32)
            for slot in slots:
                value = value + self.box[slot].astype(F32)
            halves.append(value)
        return halves


def picked(k, values):
    result = values[0]
    for n in range(1, len(values)):
        result = jnp.where(k == n, values[n], result)
    return result


def kernel(
    nz, x_ref, ng_ref, cw_ref, cb_ref, gw_ref, gb_ref, dr_ref, mg_ref, inw_hbm, outw_hbm, mi_hbm, mo_hbm, o_ref,
    xg, inw, outw, mi, wsrc, wt, acc, ss, bxs, tail, ytab, ztab, mixed, op, oi, obox, res,
    xt, acc2, ss2, hid, po, abox, bbox, abox2, bbox2, give, got, send_sem, recv_sem, local_sem,
):
    tm, cw = x_ref.shape
    hm = tm // 2
    ch = bxs.shape[1]
    d = ng_ref.shape[1]
    rm = tm // 2
    ff = wsrc.shape[1] // NY
    lanes = d // (nz * NY)
    zl = NY * lanes
    nseq = nz * NY

    s = lax.axis_index("seq")
    t = lax.axis_index("tensor")
    z, y = lax.div(s, NY), lax.rem(s, NY)
    x, c = lax.div(t, 2), lax.rem(t, 2)

    def dev(z_=None, y_=None, x_=None, c_=None):
        z_, y_ = (z if z_ is None else z_), (y if y_ is None else y_)
        x_, c_ = (x if x_ is None else x_), (c if c_ is None else c_)
        return (z_ * NY + y_, x_ * 2 + c_)

    along_x = lambda i: dev(x_=i)
    along_y = lambda j: dev(y_=j)
    sibling = dev(c_=1 - c)
    xn, xp, xo = mod(x + 1, NX), mod(x + 3, NX), mod(x + 2, NX)
    yn, yp, yo = mod(y + 1, NY), mod(y + 3, NY), mod(y + 2, NY)
    after, before = (mod(s + 1, nseq), t), (mod(s + nseq - 1, nseq), t)

    loads = {}
    for number, (name, src, dst) in enumerate(
        (("inw", inw_hbm, inw), ("outw", outw_hbm, outw), ("mi", mi_hbm, mi), ("mo", mo_hbm, wsrc.at[2]))
    ):
        loads[name] = pltpu.make_async_copy(src, dst, local_sem.at[number])
    for name in ("mi", "mo", "inw", "outw"):
        loads[name].start()

    barrier = pltpu.get_barrier_semaphore()
    partners = [dev(x_=xn), dev(x_=xp), sibling, after, before]
    partners += [dev(y_=mod(y + k, NY)) for k in range(1, NY)]
    partners += [dev(z_=mod(z + k, nz)) for k in range(1, nz)]
    for partner in partners:
        pl.semaphore_signal(barrier, inc=1, device_id=partner, device_id_type=pl.DeviceIdType.MESH)
    pl.semaphore_wait(barrier, len(partners))

    wire = Wire(send_sem, recv_sem)

    def x_piece(i, h):
        return xg.at[i * 2 + c, pl.ds(h * hm, hm)]

    xring = Spread(wire, x_piece, x, along_x, own=lambda h: x_ref.at[pl.ds(h * hm, hm)])
    xring.start()
    to_sib = {}
    for name, i in (("own", x), ("prv", xp), ("nxt", xn), ("opp", xo)):
        src = x_ref if name == "own" else xg.at[i * 2 + c]
        to_sib[name] = wire.message(src, xg.at[i * 2 + c], xg.at[i * 2 + 1 - c], sibling)
    to_sib["own"].start()
    xg[t] = x_ref[...]

    loads["mi"].wait()
    for g in range(2):
        wsrc[g] = mi[g].astype(F32).T.astype(BF16)
    loads["mo"].wait()

    def w_rows(j):
        return wsrc.at[:, pl.ds(pl.multiple_of(j * ff, 16), ff)]

    def w_lanes(slot, start, size):
        return wt.at[:, pl.ds(slot * ff, ff), pl.ds(pl.multiple_of(start, 128), size)]

    w_over_y = []
    for k in range(1, NY):
        j, src_y = mod(y + k, NY), mod(y + NY - k, NY)
        message = wire.message(
            w_rows(j), w_lanes(0, s * lanes, lanes), w_lanes(0, (z * NY + src_y) * lanes, lanes), along_y(j)
        )
        message.start()
        w_over_y.append(message)
    wt[:, pl.ds(0, ff), pl.ds(pl.multiple_of(s * lanes, 128), lanes)] = wsrc[:, pl.ds(pl.multiple_of(y * ff, 16), ff)]

    zn, zp = mod(z + 1, nz), mod(z + nz - 1, nz)
    steps = nz // 2
    z_up, z_down, w_sib = [], [], []
    for k in range(1, steps + 1):
        half = zl // 2 if k == steps else zl
        up, up_in = mod(z + nz - (k - 1), nz) * zl, mod(z + nz - k, nz) * zl
        down, down_in = mod(z + k - 1, nz) * zl, mod(z + k, nz) * zl
        shift = zl - half
        z_up.append(wire.message(w_lanes(0, up, half), w_lanes(0, up, half), w_lanes(0, up_in, half), dev(z_=zn)))
        z_down.append(
            wire.message(
                w_lanes(0, down + shift, half), w_lanes(0, down + shift, half), w_lanes(0, down_in + shift, half),
                dev(z_=zp),
            )
        )

    def w_to_sib(start, size):
        w_sib.append(wire.message(w_lanes(0, start, size), w_lanes(1, start, size), w_lanes(1, start, size), sibling))

    w_to_sib(z * zl, zl)
    for k in range(1, steps + 1):
        half = zl // 2 if k == steps else zl
        w_to_sib(mod(z + nz - k, nz) * zl, half)
        w_to_sib(mod(z + k, nz) * zl + zl - half, half)

    def weights_begin():
        for message in w_over_y:
            message.arrived()
        z_up[0].start()
        z_down[0].start()
        w_sib[0].start()

    def weights_step(k):
        z_up[k - 1].arrived()
        if k < steps:
            z_up[k].start()
        z_down[k - 1].arrived()
        if k < steps:
            z_down[k].start()
        w_sib[2 * k - 1].start()
        w_sib[2 * k].start()

    acc[...] = jnp.zeros_like(acc)
    ss[...] = jnp.zeros_like(ss)
    loads["inw"].wait()
    order = [t, x * 2 + 1 - c, xp * 2 + c, xn * 2 + c, xp * 2 + 1 - c, xn * 2 + 1 - c, xo * 2 + c, xo * 2 + 1 - c]

    def step_2():
        xring.forward()
        xring.prv_done()
        to_sib["prv"].start()

    def step_3():
        xring.nxt_done()
        to_sib["nxt"].start()

    def step_6():
        xring.opp_done()
        to_sib["opp"].start()

    arrivals = {
        1: to_sib["own"].arrived,
        2: step_2,
        3: step_3,
        4: to_sib["prv"].arrived,
        5: to_sib["nxt"].arrived,
        6: step_6,
        7: to_sib["opp"].arrived,
    }

    def take(k, _):
        for at, step in arrivals.items():
            pl.when(k == at)(step)
        b = picked(k, order)
        at = pl.multiple_of(b * cw, 128)
        block = xg[b].astype(F32)
        ss[...] += jnp.sum(block * block, axis=1, keepdims=True)
        scaled = (block * ng_ref[:, pl.ds(at, cw)]).astype(BF16)
        for g in range(2):
            acc[g] += jnp.dot(scaled, inw[g, pl.ds(at, cw)], preferred_element_type=F32)
        return 0

    lax.fori_loop(0, 8, take, 0)
    scale = lax.rsqrt(ss[...] * (1.0 / d) + EPS)
    bxs[...] = (acc[0] * scale).astype(BF16)
    tails = wire.message(bxs.at[pl.ds(tm - 16, 16)], tail, tail, after)
    tails.start()
    weights_begin()
    branch_y = jax.nn.gelu(acc[1] * scale, approximate=True)
    acc[1] = branch_y

    tails.arrived()
    earlier = jnp.where(s > 0, tail[...].astype(F32), 0.0)
    padded = jnp.concatenate([earlier, bxs[...].astype(F32)], axis=0)
    convolved = jnp.zeros((tm, ch), F32) + cb_ref[...]
    for k in range(cw_ref.shape[0]):
        convolved = convolved + cw_ref[k : k + 1] * pltpu.roll(padded, k, 0)[16:]
    conv_out = convolved.astype(BF16)
    gates = [
        jnp.dot(conv_out, gw_ref[g, 0], preferred_element_type=F32) + gb_ref[g : g + 1] for g in range(2)
    ]
    log_decay = -8.0 * jax.nn.sigmoid(gates[0]) * dr_ref[...]
    decay = jnp.exp(log_decay)
    driven = conv_out.astype(F32) * jax.nn.sigmoid(gates[1]) * jnp.sqrt(expm1_negated(2.0 * log_decay))
    row = lax.broadcasted_iota(jnp.int32, (tm, ch), 0)
    step = 1
    while step < tm:
        inside = row >= step
        driven = driven + decay * jnp.where(inside, pltpu.roll(driven, step, 0), 0.0)
        decay = decay * jnp.where(inside, pltpu.roll(decay, step, 0), 1.0)
        step *= 2
    ytab[y, 0:1] = decay[tm - 1 :]
    ytab[y, 1:2] = driven[tm - 1 :]
    over_y = []
    for k in range(1, NY):
        over_y.append(
            wire.message(ytab.at[y], ytab.at[y], ytab.at[mod(y + NY - k, NY)], along_y(mod(y + k, NY)))
        )
        over_y[-1].start()
    for message in over_y:
        message.arrived()
    total_a, total_b = jnp.ones((1, ch), F32), jnp.zeros((1, ch), F32)
    before_a, before_b = total_a, total_b
    for j in range(NY):
        a, b = ytab[j, 0:1], ytab[j, 1:2]
        before_b = jnp.where(j < y, a * before_b + b, before_b)
        before_a = jnp.where(j < y, a * before_a, before_a)
        total_b = a * total_b + b
        total_a = a * total_a
    ztab[z, 0:1] = total_a
    ztab[z, 1:2] = total_b
    over_z = []
    for k in range(1, nz):
        over_z.append(
            wire.message(ztab.at[z], ztab.at[z], ztab.at[mod(z + nz - k, nz)], dev(z_=mod(z + k, nz)))
        )
        over_z[-1].start()
    for message in over_z:
        message.arrived()
    carry = jnp.zeros((1, ch), F32)
    for j in range(nz):
        carry = jnp.where(j < z, ztab[j, 0:1] * carry + ztab[j, 1:2], carry)
    carry = before_a * carry + before_b
    mixed[...] = ((decay * carry + driven) * acc[1]).astype(BF16)
    if steps > 1:
        weights_step(1)

    loads["outw"].wait()
    columns = (xo, xn, xp, x)

    def block(i):
        return pl.ds(pl.multiple_of(i * cw, 128), cw)

    over_d2d = []
    for n, i in enumerate(columns):
        for core in (1 - c, c):
            at = pl.multiple_of((i * 2 + core) * cw, 128)
            part = jnp.dot(mixed[...], outw[:, pl.ds(at, cw)], preferred_element_type=F32)
            op[core, :, block(i)] = part.astype(BF16)
            if core is not c:
                over_d2d.append(wire.message(op.at[1 - c, :, block(i)], oi.at[n], oi.at[n], sibling))
                over_d2d[-1].start()

    out_ring = Gathered(wire, lambda i, h: op.at[c, pl.ds(h * hm, hm), block(i)], x, along_x, obox)
    starts = (out_ring.start_far, out_ring.start_next, out_ring.start_prev, lambda: None)
    for n, i in enumerate(columns):
        over_d2d[n].arrived()
        op[c, :, block(i)] = (op[c, :, block(i)].astype(F32) + oi[n].astype(F32)).astype(BF16)
        starts[n]()
    out_ring.relay()
    for h, value in enumerate(out_ring.result()):
        rows = pl.ds(h * hm, hm)
        res[rows] = (x_ref[rows].astype(F32) + value).astype(BF16)

    def token(j, h=None):
        if h is None:
            return pl.ds(pl.multiple_of(j * rm, 16), rm)
        return pl.ds(pl.multiple_of(j * rm + h * (rm // 2), 16), rm // 2)

    mine, theirs = pl.ds(pl.multiple_of(c * rm, 16), rm), pl.ds(pl.multiple_of((1 - c) * rm, 16), rm)
    swap = wire.message(
        res.at[theirs], xt.at[c, token(y), block(x)], xt.at[1 - c, token(y), block(x)], sibling,
    )
    swap.start()
    xt[c, token(y), block(x)] = res[mine]
    other = 1 - c
    a_x = Spread(wire, lambda i, h: xt.at[c, token(y, h), block(i)], x, along_x)
    a_y = [
        Spread(wire, lambda j, h, i=i: xt.at[c, token(j, h), block(i)], y, along_y) for i in (x, xp, xn, xo)
    ]
    b_y = Spread(wire, lambda j, h: xt.at[other, token(j, h), block(x)], y, along_y)
    b_x = [
        Spread(wire, lambda i, h, j=j: xt.at[other, token(j, h), block(i)], x, along_x) for j in (y, yp, yn, yo)
    ]
    a_x.start()
    a_y[0].start()
    if steps > 2:
        weights_step(2)
    swap.arrived()
    b_y.start()
    b_x[0].start()
    a_x.forward()
    b_y.forward()
    a_x.prv_done()
    a_y[1].start()
    b_y.prv_done()
    b_x[1].start()
    a_x.nxt_done()
    a_y[2].start()
    b_y.nxt_done()
    b_x[2].start()
    a_y[0].forward()
    b_x[0].forward()
    a_x.opp_done()
    a_y[3].start()
    b_y.opp_done()
    b_x[3].start()
    for k in range(3, steps):
        weights_step(k)
    acc2[...] = jnp.zeros_like(acc2)
    ss2[...] = jnp.zeros_like(ss2)

    def ring_done(ring):
        ring.prv_done()
        ring.nxt_done()
        ring.opp_done()

    def rows_0():
        a_y[1].forward()
        b_x[1].forward()
        ring_done(a_y[0])
        weights_step(steps)
        for message in w_sib:
            message.arrived()

    def rows_1():
        a_y[2].forward()
        b_x[2].forward()

    def rows_2():
        a_y[3].forward()
        b_x[3].forward()
        ring_done(a_y[1])

    def rows_3():
        ring_done(a_y[2])

    def rows_4():
        for ring in b_x:
            ring.prv_done()

    def rows_5():
        for ring in b_x:
            ring.nxt_done()

    def rows_6():
        ring_done(a_y[3])

    def rows_7():
        for ring in b_x:
            ring.opp_done()

    row_steps = (rows_0, rows_1, rows_2, rows_3, rows_4, rows_5, rows_6, rows_7)
    which = ((c, x), (other, x), (c, xp), (c, xn), (other, xp), (other, xn), (c, xo), (other, xo))

    def multiply(k, _):
        for at, step in enumerate(row_steps):
            pl.when(k == at)(step)
        core, i = picked(k, [w[0] for w in which]), picked(k, [w[1] for w in which])
        at = pl.multiple_of((i * 2 + core) * cw, 128)
        rows = xt[core, :, block(i)].astype(F32)
        ss2[...] += jnp.sum(rows * rows, axis=1, keepdims=True)
        scaled = (rows * mg_ref[:, pl.ds(at, cw)]).astype(BF16)
        for g in range(2):
            acc2[g] += lax.dot_general(
                scaled, wt[g, :, pl.ds(at, cw)], (((1,), (1,)), ((), ())), preferred_element_type=F32
            )
        return 0

    lax.fori_loop(0, 8, multiply, 0)
    scale2 = lax.rsqrt(ss2[...] * (1.0 / d) + EPS)
    hid[...] = (jax.nn.gelu(acc2[0] * scale2, approximate=True) * (acc2[1] * scale2)).astype(BF16)

    a_back = [
        Gathered(wire, lambda j, h, i=i: po.at[c, token(j, h), block(i)], y, along_y, abox.at[n])
        for n, i in enumerate(columns)
    ]
    b_rows = (yo, yn, yp, y)
    b_back = [
        Gathered(wire, lambda i, h, j=j: po.at[other, token(j, h), block(i)], x, along_x, bbox.at[n])
        for n, j in enumerate(b_rows)
    ]
    a_last = Gathered(wire, lambda i, h: po.at[c, token(y, h), block(i)], x, along_x, abox2)
    b_last = Gathered(wire, lambda j, h: po.at[other, token(j, h), block(x)], y, along_y, bbox2)

    def down_block(core, i):
        at = pl.multiple_of((i * 2 + core) * cw, 128)
        part = jnp.dot(hid[...], wt[2, :, pl.ds(at, cw)], preferred_element_type=F32)
        po[core, :, block(i)] = part.astype(BF16)

    def a_all(n):
        a_back[n].start_far()
        a_back[n].start_next()
        a_back[n].start_prev()

    def b_all(method):
        for ring in b_back:
            getattr(ring, method)()

    down_steps = {
        0: lambda: a_all(0),
        1: lambda: b_all("start_far"),
        2: lambda: a_all(1),
        3: lambda: b_all("start_next"),
        4: lambda: a_all(2),
        5: lambda: b_all("start_prev"),
        6: lambda: a_all(3),
    }

    def down(k, _):
        down_block(picked(lax.rem(k, 2), [c, other]), picked(lax.div(k, 2), list(columns)))
        for at, step in down_steps.items():
            pl.when(k == at)(step)
        return 0

    lax.fori_loop(0, 8, down, 0)

    a_starts = (a_last.start_far, a_last.start_next, a_last.start_prev, lambda: None)
    b_starts = (b_last.start_far, b_last.start_next, b_last.start_prev, lambda: None)
    for n in range(4):
        a_back[n].relay()
        b_back[n].relay()
    for n in range(4):
        for ring, start, core, rows_at, i in (
            (a_back[n], a_starts[n], c, y, columns[n]),
            (b_back[n], b_starts[n], other, b_rows[n], x),
        ):
            for h, value in enumerate(ring.result()):
                po[core, token(rows_at, h), block(i)] = value.astype(BF16)
            start()
    b_last.relay()
    a_last.relay()
    for h, value in enumerate(b_last.result()):
        give[pl.ds(h * (rm // 2), rm // 2)] = value.astype(BF16)
    back = wire.message(give, got, got, sibling)
    back.start()
    for h, value in enumerate(a_last.result()):
        rows = pl.ds(pl.multiple_of(c * rm + h * (rm // 2), 16), rm // 2)
        o_ref[rows] = (res[rows].astype(F32) + value).astype(BF16)
    back.arrived()
    o_ref[theirs] = (res[theirs].astype(F32) + got[...].astype(F32)).astype(BF16)
    wire.drain()


def shards(
    nz, layer_input, norm_gain, in_weights, conv_weight, conv_bias, gate_weights, gate_bias, decay_rate, out_weight,
    mlp_gain, mlp_in, mlp_out,
):
    tm, cw = layer_input.shape
    d, ch = in_weights.shape[1:]
    units = mlp_out.shape[0]
    ff = units // NY
    rm = tm // 2
    vmem = pl.BlockSpec(memory_space=pltpu.VMEM)
    hbm = pl.BlockSpec(memory_space=pl.ANY)
    scratch = [
        ((8, tm, cw), BF16),
        ((2, d, ch), BF16),
        ((ch, d), BF16),
        (mlp_in.shape, BF16),
        ((3, units, mlp_in.shape[1]), BF16),
        ((3, 2 * ff, d), BF16),
        ((2, tm, ch), F32),
        ((tm, 1), F32),
        ((tm, ch), BF16),
        ((16, ch), BF16),
        ((NY, 2, ch), F32),
        ((nz, 2, ch), F32),
        ((tm, ch), BF16),
        ((2, tm, NX * cw), BF16),
        ((4, tm, cw), BF16),
        ((6, tm // 2, cw), BF16),
        ((tm, cw), BF16),
        ((2, NY * rm, NX * cw), BF16),
        ((2, NY * rm, 2 * ff), F32),
        ((NY * rm, 1), F32),
        ((NY * rm, 2 * ff), BF16),
        ((2, NY * rm, NX * cw), BF16),
        ((4, 6, rm // 2, cw), BF16),
        ((4, 6, rm // 2, cw), BF16),
        ((6, rm // 2, cw), BF16),
        ((6, rm // 2, cw), BF16),
        ((rm, cw), BF16),
        ((rm, cw), BF16),
    ]
    call = pl.pallas_call(
        functools.partial(kernel, nz),
        out_shape=jax.ShapeDtypeStruct((tm, cw), BF16),
        in_specs=[vmem] * 8 + [hbm] * 4,
        out_specs=vmem,
        scratch_shapes=[pltpu.VMEM(shape, dtype) for shape, dtype in scratch]
        + [
            pltpu.SemaphoreType.DMA((MESSAGES,)),
            pltpu.SemaphoreType.DMA((MESSAGES,)),
            pltpu.SemaphoreType.DMA((4,)),
        ],
        compiler_params=pltpu.CompilerParams(
            collective_id=0, has_side_effects=True, vmem_limit_bytes=56 * 1024 * 1024
        ),
    )
    return call(
        layer_input, norm_gain[None], conv_weight, conv_bias[None], gate_weights, gate_bias, decay_rate[None],
        mlp_gain[None], in_weights, out_weight, mlp_in, mlp_out,
    )


def solution(mesh):
    return jax.shard_map(
        functools.partial(shards, mesh.shape["seq"] // NY),
        mesh=mesh,
        in_specs=(
            P("seq", "tensor"),
            P(),
            P(None, None, "tensor"),
            P(None, "tensor"),
            P("tensor"),
            P(None, "tensor", None, None),
            P(None, "tensor"),
            P("tensor"),
            P("tensor", None),
            P(),
            P(None, "seq", "tensor"),
            P("tensor", "seq"),
        ),
        out_specs=P("seq", "tensor"),
        check_vma=False,
    )
```

time: 251 us -> 120 us (0.48)
  blocking collectives: 167 us -> 0 us
  Pallas kernels: 0 us -> 118 us
  matrix products: 22.3 us -> 0 us
  between operations: 14.4 us -> 0.01 us
  other arithmetic: 13.7 us -> 0 us
  waiting for transfers between devices: 11.3 us -> 0 us
  local copies, waits for them, and re-layouts: 12.6 us -> 1.67 us
  starting transfers between devices: 9.08 us -> 0 us
    pallas_call x0 -> x1, Pallas kernels: none -> 118 us  [shards(): call(layer_input, norm_gain[None], conv_weight, conv_bias[None], gate_wei...]
    all_to_all x3 -> x0, blocking collectives: 99.1 us -> none  [the longest x2 68.7 us: summed_on_arrival(): blocks = lax.all_to_all(in_blocks(value, dim, size), axis, 0, 0, tiled=True)]
    all_gather x2 -> x0, blocking collectives: 68.4 us -> none  [the longest x1 48.6 us: side_by_side(): lax.all_gather(both, axis, axis=dim, tiled=True)]
    dot_general x5 -> x0, matrix products: 22.3 us -> none  [the longest x1 9.92 us: shards(): jnp.einsum('tr,krf->ktf', mlp_normed, lax.all_gather(mlp_in, SEQ, axis=1,...]
    all_to_all x1 -> x0, starting transfers between devices: 7.56 us -> none  [from_everyone(): return lax.all_to_all(copies, axis, split_axis=0, concat_axis=0, tiled=True)]
    all_to_all x1 -> x0, waiting for transfers between devices: 6.42 us -> none  [from_everyone(): return lax.all_to_all(copies, axis, split_axis=0, concat_axis=0, tiled=True)]
    reduce_sum x4 -> x0, other arithmetic: 5.13 us -> none  [the longest x2 4.52 us: rms_scale(): mean_square = jnp.mean(values * values, axis=-1, keepdims=True)]
    convert_element_type x5 -> x0, other arithmetic: 4.7 us -> none  [the longest x2 3.81 us: rms_scale(): return (values * lax.rsqrt(mean_square + 1e-06) * gain).astype(jnp.bfloat16)]
  transfers between devices with their start and end apart: 4 -> 0, of which waited for: 3 -> 0; matrix products, arithmetic and copies ran while one was open for 16% -> 0% of each run, Pallas kernels for 0% -> 0%
where the time goes in v1:
time: 120 us; the launch traced here: 119 us
  Pallas kernels  118 us (98%)
  local copies, waits for them, and re-layouts  1.67 us (1%)
    pallas_call x1, Pallas kernels, shards(): call(layer_input, norm_gain[None], conv_weight, conv_bias[None], gate_wei...  118 us

profile of v1, /device:TPU:1, one launch (start us, length us, event | category | flops | bytes accessed | tf_op | source)
XLA Modules:
  0.0 119.4 jit_solution(15237434719798472773)
XLA Ops:
  0.0 117.7 %shard_map.118 = bf16[256,512]{1,0:T(8,128)(2,1)} custom-call(bf16[256,512]{1,0:T(8,128)(2,1)} %x_ref.1, f32[1,4096]{1,0:T(1,128)} %bitcast.4, f32[4,256]{1,0:T(4,128)} %cw_ref.1, f32[1,256]{1,0:T(1,128)} %bitcast.6, bf16[2,1,256,256]{3,2,1,0:T(8,128)(2,1)} %gw_ref.1, f32[2,256]{1,0:T(2,128)} %gb_ref.1, f32[1,256]{1,0:T(1,128)} %bitcast.7, ...), custom_call_target="tpu_custom_call" | custom-call | tf_op jit(solution)/shard_map/pallas_call | solution.py:647
  117.7 1.7 %copy.14 = bf16[256,512]{1,0:T(8,128)(2,1)} copy(bf16[256,512]{1,0:T(8,128)(2,1)} %shard_map.118) | data formatting | bytes 524288

commit v2 on v1

--- a/solution.py
+++ b/solution.py
@@ -12,7 +12,8 @@
 EPS = 1e-06
 F32 = jnp.float32
 BF16 = jnp.bfloat16
-MESSAGES = 200
+MESSAGES = 224
+RIM = 8
 
 
 def mod(value, size):
@@ -144,6 +145,10 @@
         return halves
 
 
+def lane_sums(value):
+    return sum(value[:, at : at + 128] for at in range(128, value.shape[1], 128)) + value[:, :128]
+
+
 def picked(k, values):
     result = values[0]
     for n in range(1, len(values)):
@@ -153,18 +158,19 @@
 
 def kernel(
     nz, x_ref, ng_ref, cw_ref, cb_ref, gw_ref, gb_ref, dr_ref, mg_ref, inw_hbm, outw_hbm, mi_hbm, mo_hbm, o_ref,
-    xg, inw, outw, mi, wsrc, wt, acc, ss, bxs, tail, ytab, ztab, mixed, op, oi, obox, res,
+    xg, inw, outw, mi, wsrc, wt, acc, ss, ytab, ztab, mixed, op, oi, obox, res,
     xt, acc2, ss2, hid, po, abox, bbox, abox2, bbox2, give, got, send_sem, recv_sem, local_sem,
 ):
     tm, cw = x_ref.shape
     hm = tm // 2
-    ch = bxs.shape[1]
+    ch = gw_ref.shape[2]
     d = ng_ref.shape[1]
     rm = tm // 2
     ff = wsrc.shape[1] // NY
     lanes = d // (nz * NY)
     zl = NY * lanes
     nseq = nz * NY
+    main = pl.ds(RIM, tm)
 
     s = lax.axis_index("seq")
     t = lax.axis_index("tensor")
@@ -181,7 +187,7 @@
     sibling = dev(c_=1 - c)
     xn, xp, xo = mod(x + 1, NX), mod(x + 3, NX), mod(x + 2, NX)
     yn, yp, yo = mod(y + 1, NY), mod(y + 3, NY), mod(y + 2, NY)
-    after, before = (mod(s + 1, nseq), t), (mod(s + nseq - 1, nseq), t)
+    after, before = mod(s + 1, nseq), mod(s + nseq - 1, nseq)
 
     loads = {}
     for number, (name, src, dst) in enumerate(
@@ -192,7 +198,8 @@
         loads[name].start()
 
     barrier = pltpu.get_barrier_semaphore()
-    partners = [dev(x_=xn), dev(x_=xp), sibling, after, before]
+    partners = [dev(x_=xn), dev(x_=xp), sibling]
+    partners += [(near, mod(t + n, 8)) for near in (after, before) for n in range(8)]
     partners += [dev(y_=mod(y + k, NY)) for k in range(1, NY)]
     partners += [dev(z_=mod(z + k, nz)) for k in range(1, nz)]
     for partner in partners:
@@ -202,79 +209,118 @@
     wire = Wire(send_sem, recv_sem)
 
     def x_piece(i, h):
-        return xg.at[i * 2 + c, pl.ds(h * hm, hm)]
+        return xg.at[i * 2 + c, pl.ds(RIM + h * hm, hm)]
+
+    rims = []
+    for n in range(8):
+        rims.append(
+            wire.message(
+                x_ref.at[pl.ds(tm - RIM, RIM)], xg.at[t, pl.ds(0, RIM)], xg.at[mod(t + 8 - n, 8), pl.ds(0, RIM)],
+                (after, mod(t + n, 8)),
+            )
+        )
+        rims[-1].start()
+
+    def rim_of(b):
+        n = mod(t + 8 - b, 8)
+        pltpu.make_async_remote_copy(
+            src_ref=x_ref.at[pl.ds(tm - RIM, RIM)],
+            dst_ref=xg.at[b, pl.ds(0, RIM)],
+            send_sem=send_sem.at[n],
+            recv_sem=recv_sem.at[n],
+            device_id=(after, t),
+            device_id_type=pl.DeviceIdType.MESH,
+        ).wait_recv()
 
     xring = Spread(wire, x_piece, x, along_x, own=lambda h: x_ref.at[pl.ds(h * hm, hm)])
     xring.start()
     to_sib = {}
     for name, i in (("own", x), ("prv", xp), ("nxt", xn), ("opp", xo)):
-        src = x_ref if name == "own" else xg.at[i * 2 + c]
-        to_sib[name] = wire.message(src, xg.at[i * 2 + c], xg.at[i * 2 + 1 - c], sibling)
+        src = x_ref if name == "own" else xg.at[i * 2 + c, main]
+        to_sib[name] = wire.message(src, xg.at[i * 2 + c, main], xg.at[i * 2 + 1 - c, main], sibling)
     to_sib["own"].start()
-    xg[t] = x_ref[...]
+    xg[t, main] = x_ref[...]
 
     loads["mi"].wait()
     for g in range(2):
         wsrc[g] = mi[g].astype(F32).T.astype(BF16)
     loads["mo"].wait()
 
-    def w_rows(j):
-        return wsrc.at[:, pl.ds(pl.multiple_of(j * ff, 16), ff)]
-
-    def w_lanes(slot, start, size):
-        return wt.at[:, pl.ds(slot * ff, ff), pl.ds(pl.multiple_of(start, 128), size)]
-
-    w_over_y = []
-    for k in range(1, NY):
-        j, src_y = mod(y + k, NY), mod(y + NY - k, NY)
-        message = wire.message(
-            w_rows(j), w_lanes(0, s * lanes, lanes), w_lanes(0, (z * NY + src_y) * lanes, lanes), along_y(j)
-        )
-        message.start()
-        w_over_y.append(message)
-    wt[:, pl.ds(0, ff), pl.ds(pl.multiple_of(s * lanes, 128), lanes)] = wsrc[:, pl.ds(pl.multiple_of(y * ff, 16), ff)]
-
     zn, zp = mod(z + 1, nz), mod(z + nz - 1, nz)
     steps = nz // 2
-    z_up, z_down, w_sib = [], [], []
-    for k in range(1, steps + 1):
-        half = zl // 2 if k == steps else zl
-        up, up_in = mod(z + nz - (k - 1), nz) * zl, mod(z + nz - k, nz) * zl
-        down, down_in = mod(z + k - 1, nz) * zl, mod(z + k, nz) * zl
-        shift = zl - half
-        z_up.append(wire.message(w_lanes(0, up, half), w_lanes(0, up, half), w_lanes(0, up_in, half), dev(z_=zn)))
-        z_down.append(
-            wire.message(
-                w_lanes(0, down + shift, half), w_lanes(0, down + shift, half), w_lanes(0, down_in + shift, half),
-                dev(z_=zp),
-            )
-        )
-
-    def w_to_sib(start, size):
-        w_sib.append(wire.message(w_lanes(0, start, size), w_lanes(1, start, size), w_lanes(1, start, size), sibling))
-
-    w_to_sib(z * zl, zl)
-    for k in range(1, steps + 1):
-        half = zl // 2 if k == steps else zl
-        w_to_sib(mod(z + nz - k, nz) * zl, half)
-        w_to_sib(mod(z + k, nz) * zl + zl - half, half)
-
-    def weights_begin():
-        for message in w_over_y:
-            message.arrived()
-        z_up[0].start()
-        z_down[0].start()
-        w_sib[0].start()
-
-    def weights_step(k):
-        z_up[k - 1].arrived()
-        if k < steps:
-            z_up[k].start()
-        z_down[k - 1].arrived()
-        if k < steps:
-            z_down[k].start()
-        w_sib[2 * k - 1].start()
-        w_sib[2 * k].start()
+    assert steps > 1
+
+    class Weights:
+        def __init__(self, first, count):
+            self.group = pl.ds(first, count)
+            self.over_y, self.up, self.down = [], [[]], [[]]
+            for k in range(1, NY):
+                j, src_y = mod(y + k, NY), mod(y + NY - k, NY)
+                self.over_y.append(
+                    wire.message(
+                        self.rows(j), self.lanes(0, s * lanes, lanes), self.lanes(0, (z * NY + src_y) * lanes, lanes),
+                        along_y(j),
+                    )
+                )
+            for k in range(NY):
+                at = mod(y + NY - k, NY) * lanes
+                here = self.lanes(0, z * zl + at, lanes)
+                src = self.rows(y) if k == 0 else here
+                self.up[0].append(wire.message(src, here, self.lanes(0, zp * zl + at, lanes), dev(z_=zn)))
+                self.down[0].append(wire.message(src, here, self.lanes(0, zn * zl + at, lanes), dev(z_=zp)))
+            self.to_sib = [[self.sib(z * zl, zl)]]
+            for k in range(1, steps + 1):
+                half = zl // 2 if k == steps else zl
+                up, up_in = mod(z + nz - (k - 1), nz) * zl, mod(z + nz - k, nz) * zl
+                down, down_in = mod(z + k - 1, nz) * zl + zl - half, mod(z + k, nz) * zl + zl - half
+                if k > 1:
+                    here, there = self.lanes(0, up, half), self.lanes(0, up_in, half)
+                    self.up.append([wire.message(here, here, there, dev(z_=zn))])
+                    here, there = self.lanes(0, down, half), self.lanes(0, down_in, half)
+                    self.down.append([wire.message(here, here, there, dev(z_=zp))])
+                self.to_sib.append([self.sib(up_in, half), self.sib(down_in, half)])
+
+        def rows(self, j):
+            return wsrc.at[self.group, pl.ds(pl.multiple_of(j * ff, 16), ff)]
+
+        def lanes(self, slot, start, size):
+            return wt.at[self.group, pl.ds(slot * ff, ff), pl.ds(pl.multiple_of(start, 128), size)]
+
+        def sib(self, start, size):
+            return wire.message(self.lanes(0, start, size), self.lanes(1, start, size), self.lanes(1, start, size), sibling)
+
+        def split(self):
+            for k in (0, 2, 1):
+                self.over_y[k].start()
+
+        def first(self, k):
+            if k > 0:
+                self.over_y[k - 1].arrived()
+            self.up[0][k].start()
+            self.down[0][k].start()
+
+        def own_to_sib(self):
+            self.to_sib[0][0].start()
+
+        def step(self, k):
+            for ring, n in ((self.up, 0), (self.down, 1)):
+                for message in ring[k - 1]:
+                    message.arrived()
+                if k < steps:
+                    ring[k][0].start()
+            for message in self.to_sib[k]:
+                message.start()
+
+        def finish(self):
+            for messages in self.to_sib:
+                for message in messages:
+                    message.arrived()
+
+    w_in, w_down = Weights(0, 2), Weights(2, 1)
+    w_in.split()
+    w_in.first(0)
+    w_down.split()
+    wt[:, pl.ds(0, ff), pl.ds(pl.multiple_of(s * lanes, 128), lanes)] = wsrc[:, pl.ds(pl.multiple_of(y * ff, 16), ff)]
 
     acc[...] = jnp.zeros_like(acc)
     ss[...] = jnp.zeros_like(ss)
@@ -285,14 +331,19 @@
         xring.forward()
         xring.prv_done()
         to_sib["prv"].start()
+        w_in.first(1)
+        w_in.first(3)
 
     def step_3():
         xring.nxt_done()
         to_sib["nxt"].start()
+        w_in.first(2)
 
     def step_6():
         xring.opp_done()
         to_sib["opp"].start()
+        for k in range(NY):
+            w_down.first(k)
 
     arrivals = {
         1: to_sib["own"].arrived,
@@ -308,29 +359,27 @@
         for at, step in arrivals.items():
             pl.when(k == at)(step)
         b = picked(k, order)
+        rim_of(b)
         at = pl.multiple_of(b * cw, 128)
         block = xg[b].astype(F32)
-        ss[...] += jnp.sum(block * block, axis=1, keepdims=True)
+        ss[...] += lane_sums(block * block)
         scaled = (block * ng_ref[:, pl.ds(at, cw)]).astype(BF16)
         for g in range(2):
             acc[g] += jnp.dot(scaled, inw[g, pl.ds(at, cw)], preferred_element_type=F32)
         return 0
 
     lax.fori_loop(0, 8, take, 0)
-    scale = lax.rsqrt(ss[...] * (1.0 / d) + EPS)
-    bxs[...] = (acc[0] * scale).astype(BF16)
-    tails = wire.message(bxs.at[pl.ds(tm - 16, 16)], tail, tail, after)
-    tails.start()
-    weights_begin()
-    branch_y = jax.nn.gelu(acc[1] * scale, approximate=True)
-    acc[1] = branch_y
-
-    tails.arrived()
-    earlier = jnp.where(s > 0, tail[...].astype(F32), 0.0)
-    padded = jnp.concatenate([earlier, bxs[...].astype(F32)], axis=0)
+    scale = lax.rsqrt(jnp.sum(ss[...], axis=1, keepdims=True) * (1.0 / d) + EPS)
+    w_in.own_to_sib()
+    w_down.own_to_sib()
+    branch_x = (acc[0] * scale).astype(BF16).astype(F32)
+    known = jnp.logical_or(s > 0, lax.broadcasted_iota(jnp.int32, branch_x.shape, 0) >= RIM)
+    branch_x = jnp.where(known, branch_x, 0.0)
+    acc[1] = jax.nn.gelu(acc[1] * scale, approximate=True)
+
     convolved = jnp.zeros((tm, ch), F32) + cb_ref[...]
     for k in range(cw_ref.shape[0]):
-        convolved = convolved + cw_ref[k : k + 1] * pltpu.roll(padded, k, 0)[16:]
+        convolved = convolved + cw_ref[k : k + 1] * pltpu.roll(branch_x, k, 0)[RIM:]
     conv_out = convolved.astype(BF16)
     gates = [
         jnp.dot(conv_out, gw_ref[g, 0], preferred_element_type=F32) + gb_ref[g : g + 1] for g in range(2)
@@ -377,9 +426,9 @@
     for j in range(nz):
         carry = jnp.where(j < z, ztab[j, 0:1] * carry + ztab[j, 1:2], carry)
     carry = before_a * carry + before_b
-    mixed[...] = ((decay * carry + driven) * acc[1]).astype(BF16)
-    if steps > 1:
-        weights_step(1)
+    mixed[...] = ((decay * carry + driven) * acc[1, RIM:]).astype(BF16)
+    w_in.step(1)
+    w_down.step(1)
 
     loads["outw"].wait()
     columns = (xo, xn, xp, x)
@@ -429,12 +478,13 @@
         Spread(wire, lambda i, h, j=j: xt.at[other, token(j, h), block(i)], x, along_x) for j in (y, yp, yn, yo)
     ]
     a_x.start()
-    a_y[0].start()
-    if steps > 2:
-        weights_step(2)
     swap.arrived()
     b_y.start()
+    a_y[0].start()
     b_x[0].start()
+    for k in range(2, min(3, steps)):
+        w_in.step(k)
+        w_down.step(k)
     a_x.forward()
     b_y.forward()
     a_x.prv_done()
@@ -445,14 +495,15 @@
     a_y[2].start()
     b_y.nxt_done()
     b_x[2].start()
+    for k in range(3, steps):
+        w_in.step(k)
+        w_down.step(k)
     a_y[0].forward()
     b_x[0].forward()
     a_x.opp_done()
     a_y[3].start()
     b_y.opp_done()
     b_x[3].start()
-    for k in range(3, steps):
-        weights_step(k)
     acc2[...] = jnp.zeros_like(acc2)
     ss2[...] = jnp.zeros_like(ss2)
 
@@ -465,9 +516,8 @@
         a_y[1].forward()
         b_x[1].forward()
         ring_done(a_y[0])
-        weights_step(steps)
-        for message in w_sib:
-            message.arrived()
+        w_in.step(steps)
+        w_in.finish()
 
     def rows_1():
         a_y[2].forward()
@@ -505,7 +555,7 @@
         core, i = picked(k, [w[0] for w in which]), picked(k, [w[1] for w in which])
         at = pl.multiple_of((i * 2 + core) * cw, 128)
         rows = xt[core, :, block(i)].astype(F32)
-        ss2[...] += jnp.sum(rows * rows, axis=1, keepdims=True)
+        ss2[...] += lane_sums(rows * rows)
         scaled = (rows * mg_ref[:, pl.ds(at, cw)]).astype(BF16)
         for g in range(2):
             acc2[g] += lax.dot_general(
@@ -514,7 +564,9 @@
         return 0
 
     lax.fori_loop(0, 8, multiply, 0)
-    scale2 = lax.rsqrt(ss2[...] * (1.0 / d) + EPS)
+    w_down.step(steps)
+    w_down.finish()
+    scale2 = lax.rsqrt(jnp.sum(ss2[...], axis=1, keepdims=True) * (1.0 / d) + EPS)
     hid[...] = (jax.nn.gelu(acc2[0] * scale2, approximate=True) * (acc2[1] * scale2)).astype(BF16)
 
     a_back = [
@@ -600,16 +652,14 @@
     vmem = pl.BlockSpec(memory_space=pltpu.VMEM)
     hbm = pl.BlockSpec(memory_space=pl.ANY)
     scratch = [
-        ((8, tm, cw), BF16),
+        ((8, RIM + tm, cw), BF16),
         ((2, d, ch), BF16),
         ((ch, d), BF16),
         (mlp_in.shape, BF16),
         ((3, units, mlp_in.shape[1]), BF16),
         ((3, 2 * ff, d), BF16),
-        ((2, tm, ch), F32),
-        ((tm, 1), F32),
-        ((tm, ch), BF16),
-        ((16, ch), BF16),
+        ((2, RIM + tm, ch), F32),
+        ((RIM + tm, 128), F32),
         ((NY, 2, ch), F32),
         ((nz, 2, ch), F32),
         ((tm, ch), BF16),
@@ -619,7 +669,7 @@
         ((tm, cw), BF16),
         ((2, NY * rm, NX * cw), BF16),
         ((2, NY * rm, 2 * ff), F32),
-        ((NY * rm, 1), F32),
+        ((NY * rm, 128), F32),
         ((NY * rm, 2 * ff), BF16),
         ((2, NY * rm, NX * cw), BF16),
         ((4, 6, rm // 2, cw), BF16),

time: 120 us -> 114 us (0.950)
  Pallas kernels: 118 us -> 112 us
    pallas_call x1, Pallas kernels: 118 us -> 112 us  [shards(): call(layer_input, norm_gain[None], conv_weight, conv_bias[None], gate_wei...]
where the time goes in v2:
time: 114 us
  Pallas kernels  112 us (98%)
  local copies, waits for them, and re-layouts  1.67 us (1%)
    pallas_call x1, Pallas kernels, shards(): call(layer_input, norm_gain[None], conv_weight, conv_bias[None], gate_wei...  112 us

profile of v2, /device:TPU:1, one launch (start us, length us, event | category | flops | bytes accessed | tf_op | source)
XLA Modules:
  0.0 114.0 jit_solution(6593019789071686288)
XLA Ops:
  0.0 112.4 %shard_map.118 = bf16[256,512]{1,0:T(8,128)(2,1)} custom-call(bf16[256,512]{1,0:T(8,128)(2,1)} %x_ref.1, f32[1,4096]{1,0:T(1,128)} %bitcast.4, f32[4,256]{1,0:T(4,128)} %cw_ref.1, f32[1,256]{1,0:T(1,128)} %bitcast.6, bf16[2,1,256,256]{3,2,1,0:T(8,128)(2,1)} %gw_ref.1, f32[2,256]{1,0:T(2,128)} %gb_ref.1, f32[1,256]{1,0:T(1,128)} %bitcast.7, ...), custom_call_target="tpu_custom_call" | custom-call | tf_op jit(solution)/shard_map/pallas_call | solution.py:697
  112.4 1.7 %copy.14 = bf16[256,512]{1,0:T(8,128)(2,1)} copy(bf16[256,512]{1,0:T(8,128)(2,1)} %shard_map.118) | data formatting | bytes 524288

commit v3 on v2

--- a/solution.py
+++ b/solution.py
@@ -12,8 +12,9 @@
 EPS = 1e-06
 F32 = jnp.float32
 BF16 = jnp.bfloat16
-MESSAGES = 224
+MESSAGES = 352
 RIM = 8
+GROUPS = 2
 
 
 def mod(value, size):
@@ -29,51 +30,57 @@
 
 class Wire:
     def __init__(self, send, recv):
-        self.send, self.recv, self.used, self.open = send, recv, 0, []
+        self.send, self.recv, self.used, self.lots = send, recv, 0, []
+
+    def lot(self, whole):
+        self.lots.append(whole)
+        return Lot(self, len(self.lots) - 1)
+
+    def drain(self):
+        for number, whole in enumerate(self.lots):
+            pltpu.make_async_copy(whole, whole, self.send.at[number]).wait()
+
+
+class Lot:
+    def __init__(self, wire, number):
+        self.wire, self.number = wire, number
 
     def message(self, src, dst, landing, device):
-        self.used += 1
-        return Message(self, self.used - 1, src, dst, landing, device)
-
-    def drain(self):
-        for message in self.open:
-            message.copy(message.dst).wait_send()
+        self.wire.used += 1
+        return Message(self.wire.send.at[self.number], self.wire.recv.at[self.wire.used - 1], src, dst, landing, device)
 
 
 class Message:
-    def __init__(self, wire, number, src, dst, landing, device):
-        self.wire, self.number, self.src, self.dst, self.landing, self.device = (
-            wire, number, src, dst, landing, device,
-        )
+    def __init__(self, send, recv, src, dst, landing, device):
+        self.send, self.recv, self.src, self.dst, self.landing, self.device = send, recv, src, dst, landing, device
 
     def copy(self, dst):
         return pltpu.make_async_remote_copy(
             src_ref=self.src,
             dst_ref=dst,
-            send_sem=self.wire.send.at[self.number],
-            recv_sem=self.wire.recv.at[self.number],
+            send_sem=self.send,
+            recv_sem=self.recv,
             device_id=self.device,
             device_id_type=pl.DeviceIdType.MESH,
         )
 
     def start(self):
         self.copy(self.dst).start()
-        self.wire.open.append(self)
 
     def arrived(self):
         self.copy(self.landing).wait_recv()
 
 
 class Spread:
-    def __init__(self, wire, piece, me, device_of, own=None):
+    def __init__(self, lot, piece, me, device_of, own=None):
         nxt, prv, opp = mod(me + 1, 4), mod(me + 3, 4), mod(me + 2, 4)
         own = own or (lambda h: piece(me, h))
-        self.na = wire.message(own(0), piece(me, 0), piece(prv, 0), device_of(nxt))
-        self.nb = wire.message(own(1), piece(me, 1), piece(prv, 1), device_of(nxt))
-        self.pb = wire.message(own(1), piece(me, 1), piece(nxt, 1), device_of(prv))
-        self.pa = wire.message(own(0), piece(me, 0), piece(nxt, 0), device_of(prv))
-        self.fn = wire.message(piece(prv, 0), piece(prv, 0), piece(opp, 0), device_of(nxt))
-        self.fp = wire.message(piece(nxt, 1), piece(nxt, 1), piece(opp, 1), device_of(prv))
+        self.na = lot.message(own(0), piece(me, 0), piece(prv, 0), device_of(nxt))
+        self.nb = lot.message(own(1), piece(me, 1), piece(prv, 1), device_of(nxt))
+        self.pb = lot.message(own(1), piece(me, 1), piece(nxt, 1), device_of(prv))
+        self.pa = lot.message(own(0), piece(me, 0), piece(nxt, 0), device_of(prv))
+        self.fn = lot.message(piece(prv, 0), piece(prv, 0), piece(opp, 0), device_of(nxt))
+        self.fp = lot.message(piece(nxt, 1), piece(nxt, 1), piece(opp, 1), device_of(prv))
 
     def start(self):
         self.na.start()
@@ -99,11 +106,11 @@
 
 
 class Gathered:
-    def __init__(self, wire, part, me, device_of, box):
+    def __init__(self, lot, part, me, device_of, box):
         nxt, prv, opp = mod(me + 1, 4), mod(me + 3, 4), mod(me + 2, 4)
         self.part, self.me, self.nxt, self.prv, self.box = part, me, nxt, prv, box
         def send(src, slot, device):
-            return wire.message(src, box.at[slot], box.at[slot], device)
+            return lot.message(src, box.at[slot], box.at[slot], device)
         self.oa = send(part(opp, 0), 0, device_of(nxt))
         self.ob = send(part(opp, 1), 1, device_of(prv))
         self.db = send(part(nxt, 1), 2, device_of(nxt))
@@ -147,6 +154,15 @@
 
 def lane_sums(value):
     return sum(value[:, at : at + 128] for at in range(128, value.shape[1], 128)) + value[:, :128]
+
+
+def at_step(k, steps):
+    for number, step in steps.items():
+
+        def run(step=step):
+            step()
+
+        pl.when(k == number)(run)
 
 
 def picked(k, values):
@@ -211,10 +227,11 @@
     def x_piece(i, h):
         return xg.at[i * 2 + c, pl.ds(RIM + h * hm, hm)]
 
+    lot = wire.lot(xg.at[0, pl.ds(0, 8 * RIM)])
     rims = []
     for n in range(8):
         rims.append(
-            wire.message(
+            lot.message(
                 x_ref.at[pl.ds(tm - RIM, RIM)], xg.at[t, pl.ds(0, RIM)], xg.at[mod(t + 8 - n, 8), pl.ds(0, RIM)],
                 (after, mod(t + n, 8)),
             )
@@ -226,18 +243,19 @@
         pltpu.make_async_remote_copy(
             src_ref=x_ref.at[pl.ds(tm - RIM, RIM)],
             dst_ref=xg.at[b, pl.ds(0, RIM)],
-            send_sem=send_sem.at[n],
+            send_sem=send_sem.at[0],
             recv_sem=recv_sem.at[n],
             device_id=(after, t),
             device_id_type=pl.DeviceIdType.MESH,
         ).wait_recv()
 
-    xring = Spread(wire, x_piece, x, along_x, own=lambda h: x_ref.at[pl.ds(h * hm, hm)])
+    xring = Spread(wire.lot(obox), x_piece, x, along_x, own=lambda h: x_ref.at[pl.ds(h * hm, hm)])
     xring.start()
     to_sib = {}
+    lot = wire.lot(oi)
     for name, i in (("own", x), ("prv", xp), ("nxt", xn), ("opp", xo)):
         src = x_ref if name == "own" else xg.at[i * 2 + c, main]
-        to_sib[name] = wire.message(src, xg.at[i * 2 + c, main], xg.at[i * 2 + 1 - c, main], sibling)
+        to_sib[name] = lot.message(src, xg.at[i * 2 + c, main], xg.at[i * 2 + 1 - c, main], sibling)
     to_sib["own"].start()
     xg[t, main] = x_ref[...]
 
@@ -254,10 +272,12 @@
         def __init__(self, first, count):
             self.group = pl.ds(first, count)
             self.over_y, self.up, self.down = [], [[]], [[]]
+            self.ring = wire.lot(self.lanes(0, 0, (3 * NY - 1) * lanes + (nz - 1) * zl - 2 * zl))
+            self.pair = wire.lot(self.lanes(0, 0, d))
             for k in range(1, NY):
                 j, src_y = mod(y + k, NY), mod(y + NY - k, NY)
                 self.over_y.append(
-                    wire.message(
+                    self.ring.message(
                         self.rows(j), self.lanes(0, s * lanes, lanes), self.lanes(0, (z * NY + src_y) * lanes, lanes),
                         along_y(j),
                     )
@@ -266,8 +286,8 @@
                 at = mod(y + NY - k, NY) * lanes
                 here = self.lanes(0, z * zl + at, lanes)
                 src = self.rows(y) if k == 0 else here
-                self.up[0].append(wire.message(src, here, self.lanes(0, zp * zl + at, lanes), dev(z_=zn)))
-                self.down[0].append(wire.message(src, here, self.lanes(0, zn * zl + at, lanes), dev(z_=zp)))
+                self.up[0].append(self.ring.message(src, here, self.lanes(0, zp * zl + at, lanes), dev(z_=zn)))
+                self.down[0].append(self.ring.message(src, here, self.lanes(0, zn * zl + at, lanes), dev(z_=zp)))
             self.to_sib = [[self.sib(z * zl, zl)]]
             for k in range(1, steps + 1):
                 half = zl // 2 if k == steps else zl
@@ -275,9 +295,9 @@
                 down, down_in = mod(z + k - 1, nz) * zl + zl - half, mod(z + k, nz) * zl + zl - half
                 if k > 1:
                     here, there = self.lanes(0, up, half), self.lanes(0, up_in, half)
-                    self.up.append([wire.message(here, here, there, dev(z_=zn))])
+                    self.up.append([self.ring.message(here, here, there, dev(z_=zn))])
                     here, there = self.lanes(0, down, half), self.lanes(0, down_in, half)
-                    self.down.append([wire.message(here, here, there, dev(z_=zp))])
+                    self.down.append([self.ring.message(here, here, there, dev(z_=zp))])
                 self.to_sib.append([self.sib(up_in, half), self.sib(down_in, half)])
 
         def rows(self, j):
@@ -287,7 +307,7 @@
             return wt.at[self.group, pl.ds(slot * ff, ff), pl.ds(pl.multiple_of(start, 128), size)]
 
         def sib(self, start, size):
-            return wire.message(self.lanes(0, start, size), self.lanes(1, start, size), self.lanes(1, start, size), sibling)
+            return self.pair.message(self.lanes(0, start, size), self.lanes(1, start, size), self.lanes(1, start, size), sibling)
 
         def split(self):
             for k in (0, 2, 1):
@@ -356,8 +376,7 @@
     }
 
     def take(k, _):
-        for at, step in arrivals.items():
-            pl.when(k == at)(step)
+        at_step(k, arrivals)
         b = picked(k, order)
         rim_of(b)
         at = pl.multiple_of(b * cw, 128)
@@ -397,9 +416,10 @@
     ytab[y, 0:1] = decay[tm - 1 :]
     ytab[y, 1:2] = driven[tm - 1 :]
     over_y = []
+    lot = wire.lot(ytab.at[pl.ds(0, NY - 1)])
     for k in range(1, NY):
         over_y.append(
-            wire.message(ytab.at[y], ytab.at[y], ytab.at[mod(y + NY - k, NY)], along_y(mod(y + k, NY)))
+            lot.message(ytab.at[y], ytab.at[y], ytab.at[mod(y + NY - k, NY)], along_y(mod(y + k, NY)))
         )
         over_y[-1].start()
     for message in over_y:
@@ -415,9 +435,10 @@
     ztab[z, 0:1] = total_a
     ztab[z, 1:2] = total_b
     over_z = []
+    lot = wire.lot(ztab.at[pl.ds(0, nz - 1)])
     for k in range(1, nz):
         over_z.append(
-            wire.message(ztab.at[z], ztab.at[z], ztab.at[mod(z + nz - k, nz)], dev(z_=mod(z + k, nz)))
+            lot.message(ztab.at[z], ztab.at[z], ztab.at[mod(z + nz - k, nz)], dev(z_=mod(z + k, nz)))
         )
         over_z[-1].start()
     for message in over_z:
@@ -437,206 +458,258 @@
         return pl.ds(pl.multiple_of(i * cw, 128), cw)
 
     over_d2d = []
+    lot = wire.lot(oi)
     for n, i in enumerate(columns):
         for core in (1 - c, c):
             at = pl.multiple_of((i * 2 + core) * cw, 128)
             part = jnp.dot(mixed[...], outw[:, pl.ds(at, cw)], preferred_element_type=F32)
             op[core, :, block(i)] = part.astype(BF16)
             if core is not c:
-                over_d2d.append(wire.message(op.at[1 - c, :, block(i)], oi.at[n], oi.at[n], sibling))
+                over_d2d.append(lot.message(op.at[1 - c, :, block(i)], oi.at[n], oi.at[n], sibling))
                 over_d2d[-1].start()
 
-    out_ring = Gathered(wire, lambda i, h: op.at[c, pl.ds(h * hm, hm), block(i)], x, along_x, obox)
+    out_ring = Gathered(wire.lot(obox), lambda i, h: op.at[c, pl.ds(h * hm, hm), block(i)], x, along_x, obox)
     starts = (out_ring.start_far, out_ring.start_next, out_ring.start_prev, lambda: None)
     for n, i in enumerate(columns):
         over_d2d[n].arrived()
         op[c, :, block(i)] = (op[c, :, block(i)].astype(F32) + oi[n].astype(F32)).astype(BF16)
         starts[n]()
     out_ring.relay()
+    if steps > 2:
+        w_in.step(2)
     for h, value in enumerate(out_ring.result()):
         rows = pl.ds(h * hm, hm)
         res[rows] = (x_ref[rows].astype(F32) + value).astype(BF16)
 
-    def token(j, h=None):
-        if h is None:
-            return pl.ds(pl.multiple_of(j * rm, 16), rm)
-        return pl.ds(pl.multiple_of(j * rm + h * (rm // 2), 16), rm // 2)
-
-    mine, theirs = pl.ds(pl.multiple_of(c * rm, 16), rm), pl.ds(pl.multiple_of((1 - c) * rm, 16), rm)
-    swap = wire.message(
-        res.at[theirs], xt.at[c, token(y), block(x)], xt.at[1 - c, token(y), block(x)], sibling,
-    )
-    swap.start()
-    xt[c, token(y), block(x)] = res[mine]
+    hg = rm // GROUPS
+    hh = hg // 2
     other = 1 - c
-    a_x = Spread(wire, lambda i, h: xt.at[c, token(y, h), block(i)], x, along_x)
-    a_y = [
-        Spread(wire, lambda j, h, i=i: xt.at[c, token(j, h), block(i)], y, along_y) for i in (x, xp, xn, xo)
-    ]
-    b_y = Spread(wire, lambda j, h: xt.at[other, token(j, h), block(x)], y, along_y)
-    b_x = [
-        Spread(wire, lambda i, h, j=j: xt.at[other, token(j, h), block(i)], x, along_x) for j in (y, yp, yn, yo)
-    ]
-    a_x.start()
-    swap.arrived()
-    b_y.start()
-    a_y[0].start()
-    b_x[0].start()
-    for k in range(2, min(3, steps)):
-        w_in.step(k)
-        w_down.step(k)
-    a_x.forward()
-    b_y.forward()
-    a_x.prv_done()
-    a_y[1].start()
-    b_y.prv_done()
-    b_x[1].start()
-    a_x.nxt_done()
-    a_y[2].start()
-    b_y.nxt_done()
-    b_x[2].start()
+
+    def token(j, h):
+        return pl.ds(pl.multiple_of(j * hg + h * hh, 16), hh)
+
+    def of_core(core, g, size, h=0):
+        return pl.ds(pl.multiple_of(core * rm + g * hg + h * hh, 16), size)
+
+    here_rows = pl.ds(pl.multiple_of(y * hg, 16), hg)
+
+    class Rows:
+        def __init__(self, g):
+            self.g = g
+            there = xt.at[1 - c, g, here_rows, block(x)]
+            lot = wire.lot(xt.at[0, :, pl.ds(0, 60 * hh // (NX * GROUPS))])
+            self.swap = wire.lot(there).message(res.at[of_core(other, g, hg)], xt.at[c, g, here_rows, block(x)], there, sibling)
+            self.a_x = Spread(lot, lambda i, h: xt.at[c, g, token(y, h), block(i)], x, along_x)
+            self.a_y = [
+                Spread(lot, lambda j, h, i=i: xt.at[c, g, token(j, h), block(i)], y, along_y)
+                for i in (x, xp, xn, xo)
+            ]
+            self.b_y = Spread(lot, lambda j, h: xt.at[other, g, token(j, h), block(x)], y, along_y)
+            self.b_x = [
+                Spread(lot, lambda i, h, j=j: xt.at[other, g, token(j, h), block(i)], x, along_x)
+                for j in (y, yp, yn, yo)
+            ]
+
+        def begin(self):
+            self.swap.start()
+            xt[c, self.g, here_rows, block(x)] = res[of_core(c, self.g, hg)]
+            self.a_x.start()
+
+        def begin_other(self):
+            self.swap.arrived()
+            self.b_y.start()
+
+        def own(self):
+            self.a_y[0].start()
+            self.b_x[0].start()
+
+        def relay_first(self):
+            self.a_x.forward()
+            self.b_y.forward()
+
+        def sides(self):
+            self.a_x.prv_done()
+            self.a_y[1].start()
+            self.b_y.prv_done()
+            self.b_x[1].start()
+            self.a_x.nxt_done()
+            self.a_y[2].start()
+            self.b_y.nxt_done()
+            self.b_x[2].start()
+
+        def far(self):
+            self.a_x.opp_done()
+            self.a_y[3].start()
+            self.b_y.opp_done()
+            self.b_x[3].start()
+
+        def relay(self, n):
+            self.a_y[n].forward()
+            self.b_x[n].forward()
+
+        def a_done(self, n):
+            self.a_y[n].prv_done()
+            self.a_y[n].nxt_done()
+            self.a_y[n].opp_done()
+
+        def b_done(self, which):
+            for ring in self.b_x:
+                getattr(ring, which)()
+
+    class Sums:
+        def __init__(self, g):
+            self.g = g
+            lot = wire.lot(po.at[0, :, pl.ds(0, 60 * hh // (NX * GROUPS))])
+            self.a = [
+                Gathered(lot, lambda j, h, i=i: po.at[c, g, token(j, h), block(i)], y, along_y, abox.at[g, n])
+                for n, i in enumerate(columns)
+            ]
+            self.b = [
+                Gathered(lot, lambda i, h, j=j: po.at[other, g, token(j, h), block(i)], x, along_x, bbox.at[g, n])
+                for n, j in enumerate(b_rows)
+            ]
+            self.a_last = Gathered(lot, lambda i, h: po.at[c, g, token(y, h), block(i)], x, along_x, abox2.at[g])
+            self.b_last = Gathered(lot, lambda j, h: po.at[other, g, token(j, h), block(x)], y, along_y, bbox2.at[g])
+            self.back = wire.lot(give.at[g]).message(give.at[g], got.at[g], got.at[g], sibling)
+
+        def a_all(self, n):
+            self.a[n].start_far()
+            self.a[n].start_next()
+            self.a[n].start_prev()
+
+        def b_all(self, method):
+            for ring in self.b:
+                getattr(ring, method)()
+
+        def down(self):
+            starts = (
+                lambda: (self.a_all(0), self.b_all("start_far")),
+                lambda: (self.a_all(1), self.b_all("start_next")),
+                lambda: (self.a_all(2), self.b_all("start_prev")),
+                lambda: self.a_all(3),
+            )
+
+            def one(k, _):
+                i = picked(k, list(columns))
+                both = pl.ds(pl.multiple_of(i * 2 * cw, 128), 2 * cw)
+                part = jnp.dot(hid[...], wt[2, :, both], preferred_element_type=F32).astype(BF16)
+                for core in range(2):
+                    po[core, self.g, :, block(i)] = part[:, core * cw : (core + 1) * cw]
+                at_step(k, dict(enumerate(starts)))
+                return 0
+
+            lax.fori_loop(0, 4, one, 0)
+
+        def relay(self, n):
+            self.a[n].relay()
+            self.b[n].relay()
+
+        def first_sums(self):
+            a_starts = (self.a_last.start_far, self.a_last.start_next, self.a_last.start_prev, lambda: None)
+            b_starts = (self.b_last.start_far, self.b_last.start_next, self.b_last.start_prev, lambda: None)
+            for n in range(4):
+                for ring, start, core, rows_at, i in (
+                    (self.a[n], a_starts[n], c, y, columns[n]),
+                    (self.b[n], b_starts[n], other, b_rows[n], x),
+                ):
+                    for h, value in enumerate(ring.result()):
+                        po[core, self.g, token(rows_at, h), block(i)] = value.astype(BF16)
+                    start()
+
+        def relay_last(self):
+            self.b_last.relay()
+            self.a_last.relay()
+
+        def results(self):
+            for h, value in enumerate(self.b_last.result()):
+                give[self.g, pl.ds(h * hh, hh)] = value.astype(BF16)
+            self.back.start()
+            for h, value in enumerate(self.a_last.result()):
+                rows = of_core(c, self.g, hh, h)
+                o_ref[rows] = (res[rows].astype(F32) + value).astype(BF16)
+
+        def others(self):
+            self.back.arrived()
+            rows = of_core(other, self.g, hg)
+            o_ref[rows] = (res[rows].astype(F32) + got[self.g].astype(F32)).astype(BF16)
+
+    b_rows = (yo, yn, yp, y)
+    rows_0, rows_1 = Rows(0), Rows(1)
+    sums_0, sums_1 = Sums(0), Sums(1)
+
+    def multiply(rows, extra):
+        pairs = (((c, x), (other, x)), ((c, xp), (c, xn)), ((other, xp), (other, xn)), ((c, xo), (other, xo)))
+        waits = {
+            0: lambda: rows.a_done(0),
+            1: lambda: (rows.a_done(1), rows.a_done(2)),
+            2: lambda: (rows.b_done("prv_done"), rows.b_done("nxt_done")),
+            3: lambda: (rows.a_done(3), rows.b_done("opp_done")),
+        }
+        acc2[...] = jnp.zeros_like(acc2)
+        ss2[...] = jnp.zeros_like(ss2)
+
+        def one(k, _):
+            at_step(k, extra)
+            at_step(k, waits)
+            scaled, weights, squares = [], [], 0.0
+            for n in range(2):
+                core, i = picked(k, [w[n][0] for w in pairs]), picked(k, [w[n][1] for w in pairs])
+                at = pl.multiple_of((i * 2 + core) * cw, 128)
+                block_rows = xt[core, rows.g, :, block(i)].astype(F32)
+                squares = squares + lane_sums(block_rows * block_rows)
+                scaled.append((block_rows * mg_ref[:, pl.ds(at, cw)]).astype(BF16))
+                weights.append(wt[0:2, :, pl.ds(at, cw)].reshape(4 * ff, cw))
+            ss2[...] += squares
+            acc2[...] += lax.dot_general(
+                jnp.concatenate(scaled, axis=1), jnp.concatenate(weights, axis=1), (((1,), (1,)), ((), ())),
+                preferred_element_type=F32,
+            )
+            return 0
+
+        lax.fori_loop(0, 4, one, 0)
+        scale2 = lax.rsqrt(jnp.sum(ss2[...], axis=1, keepdims=True) * (1.0 / d) + EPS)
+        hid[...] = (jax.nn.gelu(acc2[:, : 2 * ff] * scale2, approximate=True) * (acc2[:, 2 * ff :] * scale2)).astype(BF16)
+
+    rows_0.begin()
+    rows_0.begin_other()
+    rows_0.own()
+    rows_1.begin()
+    rows_1.begin_other()
+    if steps > 2:
+        w_down.step(2)
+    rows_0.relay_first()
+    rows_0.sides()
+    rows_0.relay(0)
+    rows_0.far()
+    rows_1.relay_first()
     for k in range(3, steps):
         w_in.step(k)
+    rows_0.relay(1)
+    rows_1.own()
+    rows_0.relay(2)
+    rows_1.sides()
+    rows_0.relay(3)
+    rows_1.far()
+    w_in.step(steps)
+    for k in range(3, steps):
         w_down.step(k)
-    a_y[0].forward()
-    b_x[0].forward()
-    a_x.opp_done()
-    a_y[3].start()
-    b_y.opp_done()
-    b_x[3].start()
-    acc2[...] = jnp.zeros_like(acc2)
-    ss2[...] = jnp.zeros_like(ss2)
-
-    def ring_done(ring):
-        ring.prv_done()
-        ring.nxt_done()
-        ring.opp_done()
-
-    def rows_0():
-        a_y[1].forward()
-        b_x[1].forward()
-        ring_done(a_y[0])
-        w_in.step(steps)
-        w_in.finish()
-
-    def rows_1():
-        a_y[2].forward()
-        b_x[2].forward()
-
-    def rows_2():
-        a_y[3].forward()
-        b_x[3].forward()
-        ring_done(a_y[1])
-
-    def rows_3():
-        ring_done(a_y[2])
-
-    def rows_4():
-        for ring in b_x:
-            ring.prv_done()
-
-    def rows_5():
-        for ring in b_x:
-            ring.nxt_done()
-
-    def rows_6():
-        ring_done(a_y[3])
-
-    def rows_7():
-        for ring in b_x:
-            ring.opp_done()
-
-    row_steps = (rows_0, rows_1, rows_2, rows_3, rows_4, rows_5, rows_6, rows_7)
-    which = ((c, x), (other, x), (c, xp), (c, xn), (other, xp), (other, xn), (c, xo), (other, xo))
-
-    def multiply(k, _):
-        for at, step in enumerate(row_steps):
-            pl.when(k == at)(step)
-        core, i = picked(k, [w[0] for w in which]), picked(k, [w[1] for w in which])
-        at = pl.multiple_of((i * 2 + core) * cw, 128)
-        rows = xt[core, :, block(i)].astype(F32)
-        ss2[...] += lane_sums(rows * rows)
-        scaled = (rows * mg_ref[:, pl.ds(at, cw)]).astype(BF16)
-        for g in range(2):
-            acc2[g] += lax.dot_general(
-                scaled, wt[g, :, pl.ds(at, cw)], (((1,), (1,)), ((), ())), preferred_element_type=F32
-            )
-        return 0
-
-    lax.fori_loop(0, 8, multiply, 0)
+    w_in.finish()
+    multiply(rows_0, {n: functools.partial(rows_1.relay, n) for n in range(4)})
     w_down.step(steps)
     w_down.finish()
-    scale2 = lax.rsqrt(jnp.sum(ss2[...], axis=1, keepdims=True) * (1.0 / d) + EPS)
-    hid[...] = (jax.nn.gelu(acc2[0] * scale2, approximate=True) * (acc2[1] * scale2)).astype(BF16)
-
-    a_back = [
-        Gathered(wire, lambda j, h, i=i: po.at[c, token(j, h), block(i)], y, along_y, abox.at[n])
-        for n, i in enumerate(columns)
-    ]
-    b_rows = (yo, yn, yp, y)
-    b_back = [
-        Gathered(wire, lambda i, h, j=j: po.at[other, token(j, h), block(i)], x, along_x, bbox.at[n])
-        for n, j in enumerate(b_rows)
-    ]
-    a_last = Gathered(wire, lambda i, h: po.at[c, token(y, h), block(i)], x, along_x, abox2)
-    b_last = Gathered(wire, lambda j, h: po.at[other, token(j, h), block(x)], y, along_y, bbox2)
-
-    def down_block(core, i):
-        at = pl.multiple_of((i * 2 + core) * cw, 128)
-        part = jnp.dot(hid[...], wt[2, :, pl.ds(at, cw)], preferred_element_type=F32)
-        po[core, :, block(i)] = part.astype(BF16)
-
-    def a_all(n):
-        a_back[n].start_far()
-        a_back[n].start_next()
-        a_back[n].start_prev()
-
-    def b_all(method):
-        for ring in b_back:
-            getattr(ring, method)()
-
-    down_steps = {
-        0: lambda: a_all(0),
-        1: lambda: b_all("start_far"),
-        2: lambda: a_all(1),
-        3: lambda: b_all("start_next"),
-        4: lambda: a_all(2),
-        5: lambda: b_all("start_prev"),
-        6: lambda: a_all(3),
-    }
-
-    def down(k, _):
-        down_block(picked(lax.rem(k, 2), [c, other]), picked(lax.div(k, 2), list(columns)))
-        for at, step in down_steps.items():
-            pl.when(k == at)(step)
-        return 0
-
-    lax.fori_loop(0, 8, down, 0)
-
-    a_starts = (a_last.start_far, a_last.start_next, a_last.start_prev, lambda: None)
-    b_starts = (b_last.start_far, b_last.start_next, b_last.start_prev, lambda: None)
+    sums_0.down()
+    multiply(rows_1, {n: functools.partial(sums_0.relay, n) for n in range(4)})
+    sums_1.down()
+    sums_0.first_sums()
     for n in range(4):
-        a_back[n].relay()
-        b_back[n].relay()
-    for n in range(4):
-        for ring, start, core, rows_at, i in (
-            (a_back[n], a_starts[n], c, y, columns[n]),
-            (b_back[n], b_starts[n], other, b_rows[n], x),
-        ):
-            for h, value in enumerate(ring.result()):
-                po[core, token(rows_at, h), block(i)] = value.astype(BF16)
-            start()
-    b_last.relay()
-    a_last.relay()
-    for h, value in enumerate(b_last.result()):
-        give[pl.ds(h * (rm // 2), rm // 2)] = value.astype(BF16)
-    back = wire.message(give, got, got, sibling)
-    back.start()
-    for h, value in enumerate(a_last.result()):
-        rows = pl.ds(pl.multiple_of(c * rm + h * (rm // 2), 16), rm // 2)
-        o_ref[rows] = (res[rows].astype(F32) + value).astype(BF16)
-    back.arrived()
-    o_ref[theirs] = (res[theirs].astype(F32) + got[...].astype(F32)).astype(BF16)
+        sums_1.relay(n)
+    sums_0.relay_last()
+    sums_1.first_sums()
+    sums_0.results()
+    sums_1.relay_last()
+    sums_0.others()
+    sums_1.results()
+    sums_1.others()
     wire.drain()
 
 
@@ -648,7 +721,7 @@
     d, ch = in_weights.shape[1:]
     units = mlp_out.shape[0]
     ff = units // NY
-    rm = tm // 2
+    hg = tm // 2 // GROUPS
     vmem = pl.BlockSpec(memory_space=pltpu.VMEM)
     hbm = pl.BlockSpec(memory_space=pl.ANY)
     scratch = [
@@ -667,17 +740,17 @@
         ((4, tm, cw), BF16),
         ((6, tm // 2, cw), BF16),
         ((tm, cw), BF16),
-        ((2, NY * rm, NX * cw), BF16),
-        ((2, NY * rm, 2 * ff), F32),
-        ((NY * rm, 128), F32),
-        ((NY * rm, 2 * ff), BF16),
-        ((2, NY * rm, NX * cw), BF16),
-        ((4, 6, rm // 2, cw), BF16),
-        ((4, 6, rm // 2, cw), BF16),
-        ((6, rm // 2, cw), BF16),
-        ((6, rm // 2, cw), BF16),
-        ((rm, cw), BF16),
-        ((rm, cw), BF16),
+        ((2, GROUPS, NY * hg, NX * cw), BF16),
+        ((NY * hg, 4 * ff), F32),
+        ((NY * hg, 128), F32),
+        ((NY * hg, 2 * ff), BF16),
+        ((2, GROUPS, NY * hg, NX * cw), BF16),
+        ((GROUPS, 4, 6, hg // 2, cw), BF16),
+        ((GROUPS, 4, 6, hg // 2, cw), BF16),
+        ((GROUPS, 6, hg // 2, cw), BF16),
+        ((GROUPS, 6, hg // 2, cw), BF16),
+        ((GROUPS, hg, cw), BF16),
+        ((GROUPS, hg, cw), BF16),
     ]
     call = pl.pallas_call(
         functools.partial(kernel, nz),
@@ -686,7 +759,7 @@
         out_specs=vmem,
         scratch_shapes=[pltpu.VMEM(shape, dtype) for shape, dtype in scratch]
         + [
-            pltpu.SemaphoreType.DMA((MESSAGES,)),
+            pltpu.SemaphoreType.DMA((32,)),
             pltpu.SemaphoreType.DMA((MESSAGES,)),
             pltpu.SemaphoreType.DMA((4,)),
         ],

time: 114 us -> 105 us (0.921)
  Pallas kernels: 112 us -> 103 us
    pallas_call x1, Pallas kernels: 112 us -> 103 us  [shards(): call(layer_input, norm_gain[None], conv_weight, conv_bias[None], gate_wei...]
where the time goes in v3:
time: 105 us
  Pallas kernels  103 us (98%)
  local copies, waits for them, and re-layouts  1.67 us (2%)
    pallas_call x1, Pallas kernels, shards(): call(layer_input, norm_gain[None], conv_weight, conv_bias[None], gate_wei...  103 us

profile of v3, /device:TPU:1, one launch (start us, length us, event | category | flops | bytes accessed | tf_op | source)
XLA Modules:
  0.0 105.1 jit_solution(4187334454374439179)
XLA Ops:
  0.0 103.4 %shard_map.118 = bf16[256,512]{1,0:T(8,128)(2,1)} custom-call(bf16[256,512]{1,0:T(8,128)(2,1)} %x_ref.1, f32[1,4096]{1,0:T(1,128)} %bitcast.4, f32[4,256]{1,0:T(4,128)} %cw_ref.1, f32[1,256]{1,0:T(1,128)} %bitcast.6, bf16[2,1,256,256]{3,2,1,0:T(8,128)(2,1)} %gw_ref.1, f32[2,256]{1,0:T(2,128)} %gb_ref.1, f32[1,256]{1,0:T(1,128)} %bitcast.7, ...), custom_call_target="tpu_custom_call" | custom-call | tf_op jit(solution)/shard_map/pallas_call | solution.py:770
  103.4 1.7 %copy.14 = bf16[256,512]{1,0:T(8,128)(2,1)} copy(bf16[256,512]{1,0:T(8,128)(2,1)} %shard_map.118) | data formatting | bytes 524288

commit v4 on v3

--- a/solution.py
+++ b/solution.py
@@ -12,7 +12,7 @@
 EPS = 1e-06
 F32 = jnp.float32
 BF16 = jnp.bfloat16
-MESSAGES = 352
+ARRIVALS = 144
 RIM = 8
 GROUPS = 2
 
@@ -32,6 +32,10 @@
     def __init__(self, send, recv):
         self.send, self.recv, self.used, self.lots = send, recv, 0, []
 
+    def arrival(self):
+        self.used += 1
+        return self.recv.at[self.used - 1]
+
     def lot(self, whole):
         self.lots.append(whole)
         return Lot(self, len(self.lots) - 1)
@@ -45,9 +49,13 @@
     def __init__(self, wire, number):
         self.wire, self.number = wire, number
 
-    def message(self, src, dst, landing, device):
-        self.wire.used += 1
-        return Message(self.wire.send.at[self.number], self.wire.recv.at[self.wire.used - 1], src, dst, landing, device)
+    def message(self, src, dst, landing, device, arrival=None):
+        arrival = self.wire.arrival() if arrival is None else arrival
+        return Message(self.wire.send.at[self.number], arrival, src, dst, landing, device)
+
+
+def arrived(semaphore, whole):
+    pltpu.make_async_copy(whole, whole, semaphore).wait()
 
 
 class Message:
@@ -105,12 +113,38 @@
         self.fp.arrived()
 
 
+class Around:
+    def __init__(self, lot, piece, part, size, me, device_of, far=None):
+        nxt, prv, opp = mod(me + 1, 4), mod(me + 3, 4), mod(me + 2, 4)
+        self.near, self.size = lot.wire.arrival(), size
+        self.far = lot.wire.arrival() if far is None else far
+        self.n = lot.message(part(me), part(me), None, device_of(nxt), self.near)
+        self.p = lot.message(part(me), part(me), None, device_of(prv), self.near)
+        self.fn = lot.message(piece(prv, 0), piece(prv, 0), None, device_of(nxt), self.far)
+        self.fp = lot.message(piece(nxt, 1), piece(nxt, 1), None, device_of(prv), self.far)
+
+    def start(self):
+        self.n.start()
+        self.p.start()
+
+    def forward(self):
+        arrived(self.near, self.size(2))
+        self.fn.start()
+        self.fp.start()
+
+    def opp_done(self):
+        arrived(self.far, self.size(1))
+
+
 class Gathered:
     def __init__(self, lot, part, me, device_of, box):
         nxt, prv, opp = mod(me + 1, 4), mod(me + 3, 4), mod(me + 2, 4)
         self.part, self.me, self.nxt, self.prv, self.box = part, me, nxt, prv, box
+        self.first, self.last = lot.wire.arrival(), lot.wire.arrival()
+
         def send(src, slot, device):
-            return lot.message(src, box.at[slot], box.at[slot], device)
+            return lot.message(src, box.at[slot], None, device, self.first if slot < 2 else self.last)
+
         self.oa = send(part(opp, 0), 0, device_of(nxt))
         self.ob = send(part(opp, 1), 1, device_of(prv))
         self.db = send(part(nxt, 1), 2, device_of(nxt))
@@ -129,20 +163,14 @@
         self.da.start()
 
     def relay(self):
-        for arriving, leaving, member, half, slot in (
-            (self.oa, self.ca, self.nxt, 0, 0),
-            (self.ob, self.cb, self.prv, 1, 1),
-        ):
-            arriving.arrived()
+        arrived(self.first, self.box.at[pl.ds(0, 2)])
+        for leaving, member, half, slot in ((self.ca, self.nxt, 0, 0), (self.cb, self.prv, 1, 1)):
             ref = self.part(member, half)
             ref[...] = (ref[...].astype(F32) + self.box[slot].astype(F32)).astype(BF16)
             leaving.start()
 
     def result(self):
-        self.da.arrived()
-        self.ca.arrived()
-        self.db.arrived()
-        self.cb.arrived()
+        arrived(self.last, self.box.at[pl.ds(2, 4)])
         halves = []
         for half, slots in ((0, (4, 3)), (1, (2, 5))):
             value = self.part(self.me, half)[...].astype(F32)
@@ -282,12 +310,15 @@
                         along_y(j),
                     )
                 )
+            rise, fall = wire.arrival(), wire.arrival()
+            self.hop_1 = (rise, fall)
+            self.sib_all = wire.arrival()
             for k in range(NY):
                 at = mod(y + NY - k, NY) * lanes
                 here = self.lanes(0, z * zl + at, lanes)
                 src = self.rows(y) if k == 0 else here
-                self.up[0].append(self.ring.message(src, here, self.lanes(0, zp * zl + at, lanes), dev(z_=zn)))
-                self.down[0].append(self.ring.message(src, here, self.lanes(0, zn * zl + at, lanes), dev(z_=zp)))
+                self.up[0].append(self.ring.message(src, here, None, dev(z_=zn), rise))
+                self.down[0].append(self.ring.message(src, here, None, dev(z_=zp), fall))
             self.to_sib = [[self.sib(z * zl, zl)]]
             for k in range(1, steps + 1):
                 half = zl // 2 if k == steps else zl
@@ -307,7 +338,9 @@
             return wt.at[self.group, pl.ds(slot * ff, ff), pl.ds(pl.multiple_of(start, 128), size)]
 
         def sib(self, start, size):
-            return self.pair.message(self.lanes(0, start, size), self.lanes(1, start, size), self.lanes(1, start, size), sibling)
+            return self.pair.message(
+                self.lanes(0, start, size), self.lanes(1, start, size), None, sibling, self.sib_all
+            )
 
         def split(self):
             for k in (0, 2, 1):
@@ -324,17 +357,17 @@
 
         def step(self, k):
             for ring, n in ((self.up, 0), (self.down, 1)):
-                for message in ring[k - 1]:
-                    message.arrived()
+                if k == 1:
+                    arrived(self.hop_1[n], self.lanes(0, 0, zl))
+                else:
+                    ring[k - 1][0].arrived()
                 if k < steps:
                     ring[k][0].start()
             for message in self.to_sib[k]:
                 message.start()
 
         def finish(self):
-            for messages in self.to_sib:
-                for message in messages:
-                    message.arrived()
+            arrived(self.sib_all, self.lanes(1, 0, d))
 
     w_in, w_down = Weights(0, 2), Weights(2, 1)
     w_in.split()
@@ -416,14 +449,13 @@
     ytab[y, 0:1] = decay[tm - 1 :]
     ytab[y, 1:2] = driven[tm - 1 :]
     over_y = []
-    lot = wire.lot(ytab.at[pl.ds(0, NY - 1)])
+    lot, there = wire.lot(ytab.at[pl.ds(0, NY - 1)]), wire.arrival()
     for k in range(1, NY):
         over_y.append(
-            lot.message(ytab.at[y], ytab.at[y], ytab.at[mod(y + NY - k, NY)], along_y(mod(y + k, NY)))
+            lot.message(ytab.at[y], ytab.at[y], None, along_y(mod(y + k, NY)), there)
         )
         over_y[-1].start()
-    for message in over_y:
-        message.arrived()
+    arrived(there, ytab.at[pl.ds(0, NY - 1)])
     total_a, total_b = jnp.ones((1, ch), F32), jnp.zeros((1, ch), F32)
     before_a, before_b = total_a, total_b
     for j in range(NY):
@@ -435,14 +467,13 @@
     ztab[z, 0:1] = total_a
     ztab[z, 1:2] = total_b
     over_z = []
-    lot = wire.lot(ztab.at[pl.ds(0, nz - 1)])
+    lot, there = wire.lot(ztab.at[pl.ds(0, nz - 1)]), wire.arrival()
     for k in range(1, nz):
         over_z.append(
-            lot.message(ztab.at[z], ztab.at[z], ztab.at[mod(z + nz - k, nz)], dev(z_=mod(z + k, nz)))
+            lot.message(ztab.at[z], ztab.at[z], None, dev(z_=mod(z + k, nz)), there)
         )
         over_z[-1].start()
-    for message in over_z:
-        message.arrived()
+    arrived(there, ztab.at[pl.ds(0, nz - 1)])
     carry = jnp.zeros((1, ch), F32)
     for j in range(nz):
         carry = jnp.where(j < z, ztab[j, 0:1] * carry + ztab[j, 1:2], carry)
@@ -485,7 +516,9 @@
     hh = hg // 2
     other = 1 - c
 
-    def token(j, h):
+    def token(j, h=None):
+        if h is None:
+            return pl.ds(pl.multiple_of(j * hg, 16), hg)
         return pl.ds(pl.multiple_of(j * hg + h * hh, 16), hh)
 
     def of_core(core, g, size, h=0):
@@ -497,18 +530,28 @@
         def __init__(self, g):
             self.g = g
             there = xt.at[1 - c, g, here_rows, block(x)]
-            lot = wire.lot(xt.at[0, :, pl.ds(0, 60 * hh // (NX * GROUPS))])
+            lot = wire.lot(xt.at[0, :, pl.ds(0, 30 * hg // (NX * GROUPS))])
             self.swap = wire.lot(there).message(res.at[of_core(other, g, hg)], xt.at[c, g, here_rows, block(x)], there, sibling)
-            self.a_x = Spread(lot, lambda i, h: xt.at[c, g, token(y, h), block(i)], x, along_x)
-            self.a_y = [
-                Spread(lot, lambda j, h, i=i: xt.at[c, g, token(j, h), block(i)], y, along_y)
-                for i in (x, xp, xn, xo)
-            ]
-            self.b_y = Spread(lot, lambda j, h: xt.at[other, g, token(j, h), block(x)], y, along_y)
-            self.b_x = [
-                Spread(lot, lambda i, h, j=j: xt.at[other, g, token(j, h), block(i)], x, along_x)
-                for j in (y, yp, yn, yo)
-            ]
+            size = lambda n: xt.at[0, 0, pl.ds(0, n * hg), pl.ds(0, cw)]
+            self.b_far, self.size = wire.arrival(), size
+
+            def ring(core, rows, wholes, columns_of, me, device_of, far=None):
+                return Around(
+                    lot,
+                    lambda m, h: xt.at[core, g, rows(m, h), columns_of(m)],
+                    lambda m: xt.at[core, g, wholes(m), columns_of(m)],
+                    size, me, device_of, far,
+                )
+
+            def over_x(core, j, far=None):
+                return ring(core, lambda m, h: token(j, h), lambda m: token(j), block, x, along_x, far)
+
+            def over_y(core, i):
+                return ring(core, token, token, lambda m: block(i), y, along_y)
+
+            self.a_x, self.b_y = over_x(c, y), over_y(other, x)
+            self.a_y = [over_y(c, i) for i in (x, xp, xn, xo)]
+            self.b_x = [over_x(other, j, self.b_far) for j in (y, yp, yn, yo)]
 
         def begin(self):
             self.swap.start()
@@ -528,14 +571,9 @@
             self.b_y.forward()
 
         def sides(self):
-            self.a_x.prv_done()
-            self.a_y[1].start()
-            self.b_y.prv_done()
-            self.b_x[1].start()
-            self.a_x.nxt_done()
-            self.a_y[2].start()
-            self.b_y.nxt_done()
-            self.b_x[2].start()
+            for n in (1, 2):
+                self.a_y[n].start()
+                self.b_x[n].start()
 
         def far(self):
             self.a_x.opp_done()
@@ -548,13 +586,10 @@
             self.b_x[n].forward()
 
         def a_done(self, n):
-            self.a_y[n].prv_done()
-            self.a_y[n].nxt_done()
             self.a_y[n].opp_done()
 
-        def b_done(self, which):
-            for ring in self.b_x:
-                getattr(ring, which)()
+        def b_done(self):
+            arrived(self.b_far, self.size(4))
 
     class Sums:
         def __init__(self, g):
@@ -642,8 +677,7 @@
         waits = {
             0: lambda: rows.a_done(0),
             1: lambda: (rows.a_done(1), rows.a_done(2)),
-            2: lambda: (rows.b_done("prv_done"), rows.b_done("nxt_done")),
-            3: lambda: (rows.a_done(3), rows.b_done("opp_done")),
+            3: lambda: (rows.a_done(3), rows.b_done()),
         }
         acc2[...] = jnp.zeros_like(acc2)
         ss2[...] = jnp.zeros_like(ss2)
@@ -675,15 +709,15 @@
     rows_0.own()
     rows_1.begin()
     rows_1.begin_other()
+    rows_0.relay_first()
+    rows_0.sides()
+    rows_0.far()
+    for k in range(3, steps):
+        w_in.step(k)
+    rows_0.relay(0)
     if steps > 2:
         w_down.step(2)
-    rows_0.relay_first()
-    rows_0.sides()
-    rows_0.relay(0)
-    rows_0.far()
     rows_1.relay_first()
-    for k in range(3, steps):
-        w_in.step(k)
     rows_0.relay(1)
     rows_1.own()
     rows_0.relay(2)
@@ -760,7 +794,7 @@
         scratch_shapes=[pltpu.VMEM(shape, dtype) for shape, dtype in scratch]
         + [
             pltpu.SemaphoreType.DMA((32,)),
-            pltpu.SemaphoreType.DMA((MESSAGES,)),
+            pltpu.SemaphoreType.DMA((ARRIVALS,)),
             pltpu.SemaphoreType.DMA((4,)),
         ],
         compiler_params=pltpu.CompilerParams(

time: 105 us -> 103 us (0.981)
  Pallas kernels: 103 us -> 101 us
    pallas_call x1, Pallas kernels: 103 us -> 101 us  [shards(): call(layer_input, norm_gain[None], conv_weight, conv_bias[None], gate_wei...]
where the time goes in v4:
time: 103 us
  Pallas kernels  101 us (98%)
  local copies, waits for them, and re-layouts  1.67 us (2%)
    pallas_call x1, Pallas kernels, shards(): call(layer_input, norm_gain[None], conv_weight, conv_bias[None], gate_wei...  101 us

profile of v4, /device:TPU:1, one launch (start us, length us, event | category | flops | bytes accessed | tf_op | source)
XLA Modules:
  0.0 103.1 jit_solution(12611671463618216096)
XLA Ops:
  0.0 101.4 %shard_map.118 = bf16[256,512]{1,0:T(8,128)(2,1)} custom-call(bf16[256,512]{1,0:T(8,128)(2,1)} %x_ref.1, f32[1,4096]{1,0:T(1,128)} %bitcast.4, f32[4,256]{1,0:T(4,128)} %cw_ref.1, f32[1,256]{1,0:T(1,128)} %bitcast.6, bf16[2,1,256,256]{3,2,1,0:T(8,128)(2,1)} %gw_ref.1, f32[2,256]{1,0:T(2,128)} %gb_ref.1, f32[1,256]{1,0:T(1,128)} %bitcast.7, ...), custom_call_target="tpu_custom_call" | custom-call | tf_op jit(solution)/shard_map/pallas_call | solution.py:804
  101.4 1.7 %copy.14 = bf16[256,512]{1,0:T(8,128)(2,1)} copy(bf16[256,512]{1,0:T(8,128)(2,1)} %shard_map.118) | data formatting | bytes 524288

commit v5 on v4

--- a/solution.py
+++ b/solution.py
@@ -12,7 +12,8 @@
 EPS = 1e-06
 F32 = jnp.float32
 BF16 = jnp.bfloat16
-ARRIVALS = 144
+ARRIVALS = 128
+LOTS = 19
 RIM = 8
 GROUPS = 2
 
@@ -248,6 +249,10 @@
     partners += [dev(z_=mod(z + k, nz)) for k in range(1, nz)]
     for partner in partners:
         pl.semaphore_signal(barrier, inc=1, device_id=partner, device_id_type=pl.DeviceIdType.MESH)
+    loads["mi"].wait()
+    for g in range(2):
+        wsrc[g] = mi[g].astype(F32).T.astype(BF16)
+    loads["mo"].wait()
     pl.semaphore_wait(barrier, len(partners))
 
     wire = Wire(send_sem, recv_sem)
@@ -286,11 +291,6 @@
         to_sib[name] = lot.message(src, xg.at[i * 2 + c, main], xg.at[i * 2 + 1 - c, main], sibling)
     to_sib["own"].start()
     xg[t, main] = x_ref[...]
-
-    loads["mi"].wait()
-    for g in range(2):
-        wsrc[g] = mi[g].astype(F32).T.astype(BF16)
-    loads["mo"].wait()
 
     zn, zp = mod(z + 1, nz), mod(z + nz - 1, nz)
     steps = nz // 2
@@ -732,7 +732,8 @@
     w_down.step(steps)
     w_down.finish()
     sums_0.down()
-    multiply(rows_1, {n: functools.partial(sums_0.relay, n) for n in range(4)})
+    multiply(rows_1, {n + 1: functools.partial(sums_0.relay, n) for n in range(3)})
+    sums_0.relay(3)
     sums_1.down()
     sums_0.first_sums()
     for n in range(4):
@@ -793,7 +794,7 @@
         out_specs=vmem,
         scratch_shapes=[pltpu.VMEM(shape, dtype) for shape, dtype in scratch]
         + [
-            pltpu.SemaphoreType.DMA((32,)),
+            pltpu.SemaphoreType.DMA((LOTS,)),
             pltpu.SemaphoreType.DMA((ARRIVALS,)),
             pltpu.SemaphoreType.DMA((4,)),
         ],

time: 103 us -> 103 us (level)
  no operation moved by 1% of the time
where the time goes in v5:
time: 103 us
  Pallas kernels  101 us (98%)
  local copies, waits for them, and re-layouts  1.67 us (2%)
    pallas_call x1, Pallas kernels, shards(): call(layer_input, norm_gain[None], conv_weight, conv_bias[None], gate_wei...  101 us

profile of v5, /device:TPU:1, one launch (start us, length us, event | category | flops | bytes accessed | tf_op | source)
XLA Modules:
  0.0 102.7 jit_solution(15023256003771927406)
XLA Ops:
  0.0 101.0 %shard_map.118 = bf16[256,512]{1,0:T(8,128)(2,1)} custom-call(bf16[256,512]{1,0:T(8,128)(2,1)} %x_ref.1, f32[1,4096]{1,0:T(1,128)} %bitcast.4, f32[4,256]{1,0:T(4,128)} %cw_ref.1, f32[1,256]{1,0:T(1,128)} %bitcast.6, bf16[2,1,256,256]{3,2,1,0:T(8,128)(2,1)} %gw_ref.1, f32[2,256]{1,0:T(2,128)} %gb_ref.1, f32[1,256]{1,0:T(1,128)} %bitcast.7, ...), custom_call_target="tpu_custom_call" | custom-call | tf_op jit(solution)/shard_map/pallas_call | solution.py:805
  101.0 1.7 %copy.14 = bf16[256,512]{1,0:T(8,128)(2,1)} copy(bf16[256,512]{1,0:T(8,128)(2,1)} %shard_map.118) | data formatting | bytes 524288
